TPU v7x, 256 devices: a whole 4x4x8 slice. The times are simulated.
256 devices in a mesh: gy: 32 (over z, x), gx: 8 (over y, core).
Axes of the slice: x: 4, y: 4, z: 8, core: 2. Of those that a mesh axis runs over, the one named last changes fastest.
Arguments:
- right_side: float32 [32, 2048, 1024], P(None, 'gy', 'gx'), may hold values from -32 to 32
- couplings: float32 [3, 2048, 1024], P(None, 'gy', 'gx'), may hold values from 0.1 to 0.5
- center: float32 [2048, 1024], P('gy', 'gx'), may hold values from 0.6 to 1.5
- ocean_mask: int32 [2048, 1024], P('gy', 'gx'), may hold values 0 or 1
Outputs:
- solution: float32 [32, 2048, 1024], P(None, 'gy', 'gx')
- residual: float32 [32, 2048, 1024], P(None, 'gy', 'gx')
All inputs are finite; a program needn't handle non-finite values. No bound on the sum of `ocean_mask` on one device may be relied on, other than what follows from the above.
Results may differ from a plain program's by a relative error of at most 0.0055.
Values sent between devices are 32-bit elements; how exact they have to be, the bound alone decides.
No kernel may reach another device: no remote copies, remote signals or barrier semaphores. Data moves between devices by JAX's collectives and lax.ppermute only.
A program may use at most 64 MiB of HBM per device.

v0:
```python
import jax
import jax.numpy as jnp
from jax import lax
from jax.experimental import pallas as pl
from jax.experimental.pallas import tpu as pltpu
from jax.sharding import Mesh
from jax.sharding import PartitionSpec as P

ITERS = 6
SHIFT = (0.375, 0.0, 0.375, 0.0, 0.375, 0.0)
GY = ("gy_0", "gy_1")
GX = ("gx_0", "gx_1")
ALL = GY + GX
MEMBERS = 32
ROWS = 64
LANES = 128
HALO = 8
TILES = (ROWS + 2 * HALO) // 8
EXT = ROWS + 2 * HALO
GROUPS = MEMBERS // 4
PLANES = 4
BASIS = ITERS + 1
PAIRS = [(i, j) for i in range(ITERS) for j in range(i, BASIS)]
INTERPRET = False
F32 = jnp.float32
VMEM = pl.BlockSpec(memory_space=pltpu.VMEM)
SMEM = pl.BlockSpec(memory_space=pltpu.SMEM)


def lanes_of():
    return lax.broadcasted_iota(jnp.int32, (8, LANES), 1)


def slot_of(member):
    return 32 * (member % 4) + 8 * (member // 4 % 4)


def pack_kernel(right_ref, planes_ref, south_ref, north_ref, fold_ref, west_ref, east_ref, ghost_ref):
    window = lanes_of() // 8

    def one(load, tile):
        for h in range(3):
            members = range(16 * h, 16 * h + 16) if h < 2 else range(MEMBERS, MEMBERS + PLANES)
            first = last = None
            for m in members:
                value = load(m)
                slot = slot_of(m) if h < 2 else 32 * (m - MEMBERS)
                low = value if slot == 0 else pltpu.roll(value, slot, 1)
                high = pltpu.roll(value, (slot + 8) % LANES, 1)
                if first is None:
                    first, last = low, high
                else:
                    first = jnp.where(window == slot // 8, low, first)
                    last = jnp.where(window == slot // 8, high, last)
            west_ref[h, tile] = first
            east_ref[h, tile] = last

    def own(t, _):
        at = pl.multiple_of(8 * t, 8)

        def load(m):
            if m < MEMBERS:
                return right_ref[m, pl.ds(at, 8), :]
            return planes_ref[m - MEMBERS, pl.ds(at, 8), :]

        one(load, t + 1)
        return 0

    lax.fori_loop(0, ROWS // 8, own, 0)
    one(lambda m: south_ref[m], 0)

    def north(m):
        value = north_ref[m] + fold_ref[m]
        ghost_ref[m] = value
        return value

    one(north, TILES - 1)


def basis_kernel(
    top_ref, right_ref, planes_ref, south_ref, north_ref, own_west_ref, own_east_ref, from_west_ref, from_east_ref,
    basis_ref, diag_ref, gram_ref,
    strip_ref, plane_ref, plane_strip_ref, weight_ref, weight_strip_ref, inverse_ref, inverse_strip_ref, partial_ref,
):
    lane = lanes_of()
    spot = lane % 32

    def main_row(member, tile):
        return 8 + member * EXT + 8 * tile

    zero = jnp.zeros((8, LANES), F32)
    for j in range(ITERS):
        basis_ref[j, 0:8] = zero
        basis_ref[j, 8 + MEMBERS * EXT : 16 + MEMBERS * EXT] = zero
        strip_ref[j, 0:8] = zero
        strip_ref[j, 8 + GROUPS * EXT : 16 + GROUPS * EXT] = zero

    for p in range(PLANES):
        base = 8 + p * EXT
        plane_ref[base : base + 8] = south_ref[MEMBERS + p]
        plane_ref[base + 8 : base + 8 + ROWS] = planes_ref[p]
        plane_ref[base + 8 + ROWS : base + EXT] = north_ref[MEMBERS + p]
    plane_ref[0:8] = zero
    plane_ref[8 + PLANES * EXT : 16 + PLANES * EXT] = zero
    plane_strip_ref[0:8] = zero
    plane_strip_ref[8 + PLANES * EXT : 16 + PLANES * EXT] = zero

    def joined(h, tile, at):
        def moved(value, shift):
            shift %= LANES
            return value if shift == 0 else pltpu.roll(value, shift, 1)

        out = moved(from_west_ref[h, tile], -at)
        out = jnp.where(spot < 8, out, moved(own_west_ref[h, tile], 8 - at))
        out = jnp.where(spot < 16, out, moved(own_east_ref[h, tile], 16 - at))
        return jnp.where(spot < 24, out, moved(from_east_ref[h, tile], 24 - at))

    def plane_strips(t, _):
        value = joined(2, t, 0)
        for p in range(PLANES):
            one = jnp.where(lane // 32 == p, value, 0.0)
            one = one + pltpu.roll(one, 32, 1)
            one = one + pltpu.roll(one, 64, 1)
            plane_strip_ref[pl.ds(pl.multiple_of(8 + p * EXT + 8 * t, 8), 8), :] = one
        return 0

    lax.fori_loop(0, TILES, plane_strips, 0)

    def weights(t, ghost):
        dr = 1 if ghost else -1

        def row(ref, p, shift):
            return ref[pl.ds(8 + p * EXT + 8 * t + shift, 8), :]

        def beside(main, strip):
            if ghost:
                return jnp.where(lane == 127, pltpu.roll(strip, 127 - 24, 1), pltpu.roll(main, 127, 1))
            return jnp.where(lane == 0, pltpu.roll(strip, LANES - 7, 1), pltpu.roll(main, 1, 1))

        def finish(cn0, cnr, ce0, cec, cc0, ccr, ccc, ccrc, center, weight, inverse, main):
            total = center + cn0 + cnr + ce0 + cec + cc0 + ccr + ccc + ccrc
            inv = jnp.where(center > 0.0, 1.0 / total, 0.0)
            inverse[t] = inv
            if ghost:
                w = dict(s=cn0, n=cnr, w=ce0, e=cec, sw=cc0, nw=ccr, se=ccc, ne=ccrc)
            else:
                w = dict(n=cn0, s=cnr, e=ce0, w=cec, ne=cc0, se=ccr, nw=ccc, sw=ccrc)

            def ahead(value):
                value = pltpu.roll(value * inv, 1, 1)
                return jnp.where(lane == 0, 0.0, value) if main else value

            def behind(value):
                value = pltpu.roll(value * inv, LANES - 1, 1)
                return jnp.where(lane == LANES - 1, 0.0, value) if main else value

            for k, value in enumerate((
                w["s"] * inv, w["n"] * inv,
                ahead(w["se"]), ahead(w["e"]), ahead(w["ne"]),
                behind(w["sw"]), behind(w["w"]), behind(w["nw"]),
            )):
                weight[t, k] = value
            return total

        strips = [row(plane_strip_ref, p, 0) for p in range(PLANES)]
        strips_r = [row(plane_strip_ref, p, dr) for p in (0, 2)]
        side = LANES - 1 if ghost else 1
        finish(
            strips[0], strips_r[0], strips[1], pltpu.roll(strips[1], side, 1),
            strips[2], strips_r[1], pltpu.roll(strips[2], side, 1), pltpu.roll(strips_r[1], side, 1),
            strips[3], weight_strip_ref, inverse_strip_ref, False,
        )
        mains = [row(plane_ref, p, 0) for p in range(PLANES)]
        mains_r = [row(plane_ref, p, dr) for p in (0, 2)]
        return finish(
            mains[0], mains_r[0], mains[1], beside(mains[1], strips[1]),
            mains[2], mains_r[1], beside(mains[2], strips[2]), beside(mains_r[1], strips_r[1]),
            mains[3], weight_ref, inverse_ref, True,
        )

    weights(0, False)

    def inner_weights(t, _):
        diag_ref[pl.ds(pl.multiple_of(8 * (t - 1), 8), 8), :] = weights(t, False)
        return 0

    lax.fori_loop(1, TILES - 1, inner_weights, 0)

    @pl.when(top_ref[0] == 0)
    def _():
        weights(TILES - 1, False)

    @pl.when(top_ref[0] != 0)
    def _():
        weights(TILES - 1, True)

    def first(t, load):
        inv = inverse_ref[t]
        for m in range(MEMBERS):
            basis_ref[0, pl.ds(pl.multiple_of(main_row(m, t), 8), 8), :] = load(m) * inv
        inv = inverse_strip_ref[t]
        for s in range(GROUPS):
            strip_ref[0, pl.ds(pl.multiple_of(8 + s * EXT + 8 * t, 8), 8), :] = joined(s // 4, t, 8 * (s % 4)) * inv

    first(0, lambda m: south_ref[m])

    def inner_first(t, _):
        first(t, lambda m: right_ref[m, pl.ds(pl.multiple_of(8 * (t - 1), 8), 8), :])
        return 0

    lax.fori_loop(1, TILES - 1, inner_first, 0)
    first(TILES - 1, lambda m: north_ref[m])

    def step(j, t, strips):
        w = [weight_ref[t, k] for k in range(8)]
        ws = [weight_strip_ref[t, k] for k in range(8)]

        def parts(ref, base, w):
            a = ref[j, pl.ds(base - 1, 8), :]
            b = ref[j, pl.ds(pl.multiple_of(base, 8), 8), :]
            c = ref[j, pl.ds(base + 1, 8), :]
            middle = w[0] * a + w[1] * c
            if SHIFT[j]:
                middle = middle - SHIFT[j] * b
            return middle, (w[2] * a + w[4] * c) + w[3] * b, (w[5] * a + w[7] * c) + w[6] * b

        for s in range(GROUPS):
            base = 8 + s * EXT + 8 * t
            middle, ahead, behind = parts(strip_ref, base, ws)
            if strips:
                strip_ref[j + 1, pl.ds(pl.multiple_of(base, 8), 8), :] = (
                    middle + pltpu.roll(ahead, LANES - 1, 1) + pltpu.roll(behind, 1, 1)
                )
            edge = jnp.where(spot == 6, pltpu.roll(ahead, LANES - 18, 1), behind)
            for q in range(4):
                m = 4 * s + q
                base = main_row(m, t)
                middle, ahead, behind = parts(basis_ref, base, w)
                across = pltpu.roll(edge, (LANES - 7 - 32 * q) % LANES, 1)
                middle = middle + jnp.where((lane == 0) | (lane == LANES - 1), across, 0.0)
                basis_ref[j + 1, pl.ds(pl.multiple_of(base, 8), 8), :] = (
                    middle + pltpu.roll(ahead, LANES - 1, 1) + pltpu.roll(behind, 1, 1)
                )

    for j in range(ITERS - 1):
        def body(t, _, j=j):
            step(j, t, True)
            return 0

        lax.fori_loop(0, TILES, body, 0)

    def last_body(t, _):
        step(ITERS - 1, t, False)
        return 0

    lax.fori_loop(1, TILES - 1, last_body, 0)

    def products(m, _):
        sums = [None] * len(PAIRS)
        for t in range(1, TILES - 1):
            u = [basis_ref[j, pl.ds(pl.multiple_of(main_row(m, t), 8), 8), :] for j in range(BASIS)]
            d = diag_ref[8 * (t - 1) : 8 * t]
            scaled = [d * u[j] for j in range(ITERS)]
            for n, (i, j) in enumerate(PAIRS):
                term = scaled[i] * u[j]
                sums[n] = term if sums[n] is None else sums[n] + term
        for n in range(len(PAIRS)):
            partial_ref[pl.ds(pl.multiple_of((n * MEMBERS + m) * 8, 8), 8), :] = sums[n]
        return 0

    lax.fori_loop(0, MEMBERS, products, 0)
    result = zero
    for l in range(len(PAIRS) * MEMBERS // 8):
        rows = [partial_ref[pl.ds(64 * l + k, 8, stride=8), :] for k in range(8)]
        while len(rows) > 1:
            rows = [rows[k] + rows[k + 1] for k in range(0, len(rows), 2)]
        result = jnp.where(lane == l, jnp.sum(rows[0], axis=1, keepdims=True), result)
    gram_ref[...] = result


def two_sum(a, b):
    s = a + b
    t = s - a
    return s, (a - (s - t)) + (b - t)


def quick(a, b):
    s = a + b
    return s, b - (s - a)


def halves(a):
    t = 4097.0 * a
    high = t - (t - a)
    return high, a - high


def add2(a, b):
    s, e = two_sum(a[0], b[0])
    return quick(s, e + (a[1] + b[1]))


def mul2(a, b):
    p = a[0] * b[0]
    ah, al = halves(a[0])
    bh, bl = halves(b[0])
    e = ((ah * bh - p) + ah * bl + al * bh) + al * bl
    return quick(p, e + (a[0] * b[1] + a[1] * b[0]))


def neg2(a):
    return -a[0], -a[1]


def div2(a, b):
    q = a[0] / b[0]
    zero = jnp.zeros_like(q)
    rest = add2(a, neg2(mul2((q, zero), b)))
    return quick(q, rest[0] / b[0])


def sum2(terms):
    terms = list(terms)
    while len(terms) > 1:
        terms = [add2(terms[k], terms[k + 1]) if k + 1 < len(terms) else terms[k] for k in range(0, len(terms), 2)]
    return terms[0]


def finish_kernel(total_ref, basis_ref, diag_ref, solution_ref, residual_ref, coeff_ref):
    count = total_ref.shape[0]
    high, low = sum2([(total_ref[n, 0], total_ref[n, 1]) for n in range(count)])
    gram = {}
    for n, (i, j) in enumerate(PAIRS):
        shift = (LANES - 4 * n) % LANES
        value = (high, low) if shift == 0 else (pltpu.roll(high, shift, 1), pltpu.roll(low, shift, 1))
        gram[i, j] = gram[j, i] = value

    def scaled(value, factor):
        if factor == 1.0:
            return value
        s, e = two_sum(0.5 * value[0], 0.125 * value[0])
        return quick(s, e + factor * value[1])

    def product(a, b):
        terms = []
        for i, ai in enumerate(a):
            terms.append(mul2(ai, sum2([mul2(gram[i, j], bj) for j, bj in enumerate(b)])))
        return sum2(terms)

    one = (jnp.ones((8, LANES), F32), jnp.zeros((8, LANES), F32))
    precond, direction, answer = [one], [one], []
    rz = gram[0, 0]
    for k in range(ITERS):
        image = [scaled(c, 1.0 - SHIFT[j]) for j, c in enumerate(direction)]
        image = [image[0]] + [
            add2(image[j], neg2(direction[j - 1])) for j in range(1, k + 1)
        ] + [neg2(direction[k])]
        step_size = div2(rz, product(direction, image))
        moved = [mul2(step_size, c) for c in direction]
        answer = [add2(a, b) for a, b in zip(answer, moved)] + moved[len(answer):]
        moved = [neg2(mul2(step_size, c)) for c in image]
        precond = [add2(a, b) for a, b in zip(precond, moved)] + moved[len(precond):]
        if k + 1 < ITERS:
            rz_new = product(precond, precond)
            ratio = div2(rz_new, rz)
            moved = [mul2(ratio, c) for c in direction]
            direction = [add2(a, b) for a, b in zip(precond, moved)] + precond[len(moved):]
            rz = rz_new

    values = [c[0] for c in answer] + [c[0] for c in precond]
    for n, value in enumerate(values):
        for l in range(MEMBERS // 8):
            coeff_ref[n, 8 * l : 8 * l + 8] = jnp.broadcast_to(value[:, l : l + 1], (8, LANES))

    def combine(m, _):
        c = [jnp.broadcast_to(coeff_ref[n, pl.ds(m, 1), :], (8, LANES)) for n in range(2 * ITERS + 1)]
        for t in range(ROWS // 8):
            at = pl.multiple_of(16 + m * EXT + 8 * t, 8)
            u = [basis_ref[j, pl.ds(at, 8), :] for j in range(BASIS)]
            solved = c[0] * u[0]
            left = c[ITERS] * u[0]
            for j in range(1, BASIS):
                if j < ITERS:
                    solved = solved + c[j] * u[j]
                left = left + c[ITERS + j] * u[j]
            solution_ref[m, 8 * t : 8 * t + 8] = solved
            residual_ref[m, 8 * t : 8 * t + 8] = diag_ref[8 * t : 8 * t + 8] * left
        return 0

    lax.fori_loop(0, MEMBERS, combine, 0)


def shape(*dims):
    return jax.ShapeDtypeStruct(dims, F32)


def call(kernel, inputs, out_shape, scratch=(), name=None, in_specs=None):
    return pl.pallas_call(
        kernel,
        out_shape=out_shape,
        in_specs=in_specs or [VMEM] * len(inputs),
        out_specs=[VMEM] * len(out_shape),
        scratch_shapes=list(scratch),
        interpret=INTERPRET,
        name=name,
        compiler_params=pltpu.CompilerParams(vmem_limit_bytes=60 * 1024 * 1024),
    )(*inputs)


def from_everyone(value, axis):
    peers = lax.axis_size(axis)
    return lax.all_to_all(jnp.broadcast_to(value[None], (peers, *value.shape)), axis, 0, 0, tiled=True)


def on_device(right_side, couplings, center, ocean_mask):
    ny, nx = lax.axis_size(GY), lax.axis_size(GX)
    is_top = (lax.axis_index(GY) == ny - 1).astype(jnp.int32).reshape(1)
    planes = jnp.concatenate([couplings, jnp.where(ocean_mask != 0, center, 0.0)[None]], axis=0)
    last = jnp.concatenate([right_side[:, -HALO:], planes[:, -HALO:]], axis=0)
    first = jnp.concatenate([right_side[:, :HALO], planes[:, :HALO]], axis=0)
    south = lax.ppermute(last, GY, [(k, k + 1) for k in range(ny - 1)])
    north = lax.ppermute(first, GY, [(k + 1, k) for k in range(ny - 1)])
    row = (ny - 1) * nx
    fold = lax.ppermute(last[:, ::-1, ::-1], ALL, [(row + k, row + nx - 1 - k) for k in range(nx)])

    packed = shape(3, TILES, 8, LANES)
    own_west, own_east, north = call(
        pack_kernel, (right_side, planes, south, north, fold), (packed, packed, shape(MEMBERS + PLANES, 8, LANES)),
        name="pack",
    )
    from_west = lax.ppermute(own_east, GX, [(k, (k + 1) % nx) for k in range(nx)])
    from_east = lax.ppermute(own_west, GX, [((k + 1) % nx, k) for k in range(nx)])

    size = 16 + MEMBERS * EXT
    basis, diag, gram = call(
        basis_kernel,
        (is_top, right_side, planes, south, north, own_west, own_east, from_west, from_east),
        (shape(BASIS, size, LANES), shape(ROWS, LANES), shape(8, LANES)),
        scratch=(
            pltpu.VMEM((ITERS, 16 + GROUPS * EXT, LANES), F32),
            pltpu.VMEM((16 + PLANES * EXT, LANES), F32),
            pltpu.VMEM((16 + PLANES * EXT, LANES), F32),
            pltpu.VMEM((TILES, 8, 8, LANES), F32),
            pltpu.VMEM((TILES, 8, 8, LANES), F32),
            pltpu.VMEM((TILES, 8, LANES), F32),
            pltpu.VMEM((TILES, 8, LANES), F32),
            pltpu.VMEM((len(PAIRS) * MEMBERS * 8, LANES), F32),
        ),
        name="basis",
        in_specs=[SMEM] + [VMEM] * 8,
    )
    parts = from_everyone(gram, GX)
    zero = jnp.zeros((8, LANES), F32)
    near = jnp.stack(sum2([(parts[k], zero) for k in range(nx)]))
    total = from_everyone(near, GY)
    return tuple(call(
        finish_kernel,
        (total, basis, diag),
        (shape(MEMBERS, ROWS, LANES), shape(MEMBERS, ROWS, LANES)),
        scratch=(pltpu.VMEM((2 * ITERS + 1, MEMBERS, LANES), F32),),
        name="finish",
    ))


def solution(mesh):
    split = Mesh(mesh.devices.reshape(8, 4, 4, 2), ("gy_0", "gy_1", "gx_0", "gx_1"))
    placed = (P(None, GY, GX), P(None, GY, GX), P(GY, GX), P(GY, GX))
    return jax.shard_map(
        on_device,
        mesh=split,
        in_specs=placed,
        out_specs=(P(None, GY, GX), P(None, GY, GX)),
        check_vma=False,
    )
```

profile of v0, /device:TPU:1, one launch (start us, length us, event | category | flops | bytes accessed | tf_op | source)
XLA Modules:
  0.0 93.7 jit_solution(12174110199523284377)
XLA Ops:
  0.6 1.0 %fusion.12 = (f32[32,8,128]{2,1,0:T(8,128)S(1)}, f32[32,8,128]{2,1,0:T(8,128)S(1)}) fusion(f32[32,64,128]{2,1,0:T(8,128)} %right_ref.3), kind=kLoop, calls=%fused_computation.31 | loop fusion | bytes 524288 | tf_op jit(solution)/shard_map/slice | solution.py:420
  1.6 0.8 select_bitcast_fusion
  2.4 0.7 fusion.1
  3.1 3.9 %collective-permute-start = (f32[36,8,128]{2,1,0:T(8,128)S(1)}, f32[36,8,128]{2,1,0:T(8,128)S(1)}, u32[]{:S(2)}, u32[]{:S(2)}) collective-permute-start(f32[36,8,128]{2,1,0:T(8,128)S(1)} %pad_maximum_fusion.1), channel_id=1, source_target_pairs={{0,8},{8,16},{16,24},{24,32},{32,40},{40,48},{48,56},{56,64},{64,7... | collective-permute-start | bytes 442376 | tf_op jit(solution)/shard_map/ppermute | solution.py:421
  7.1 0.1 rev.3
  7.2 0.7 collective-permute-start.2
  7.9 1.3 %collective-permute-start.1 = (f32[36,8,128]{2,1,0:T(8,128)S(1)}, f32[36,8,128]{2,1,0:T(8,128)S(1)}, u32[]{:S(2)}, u32[]{:S(2)}) collective-permute-start(f32[36,8,128]{2,1,0:T(8,128)S(1)} %pad_maximum_fusion.2), channel_id=1, source_target_pairs={{8,0},{16,8},{24,16},{32,24},{40,32},{48,40},{56,48},{64,56},{72,6... | collective-permute-start | bytes 442376 | tf_op jit(solution)/shard_map/ppermute | solution.py:422
  9.2 1.6 %pad_maximum_fusion.planes_ref = f32[4,64,128]{2,1,0:T(8,128)} fusion(f32[1,64,128]{2,1,0:T(8,128)S(1)} %select_bitcast_fusion, f32[3,64,128]{2,1,0:T(8,128)} %param.5), kind=kLoop, calls=%fused_computation.2 | loop fusion | flops 32768 | bytes 262144 | tf_op jit(solution)/shard_map/concatenate | solution.py:418
  10.8 0.0 collective-permute-done.2.fold_ref
  10.8 0.0 collective-permute-done.south_ref
  10.8 0.0 copy-start
  10.8 3.5 %collective-permute-done.1.north_ref = f32[36,8,128]{2,1,0:T(8,128)S(1)} collective-permute-done((f32[36,8,128]{2,1,0:T(8,128)S(1)}, f32[36,8,128]{2,1,0:T(8,128)S(1)}, u32[]{:S(2)}, u32[]{:S(2)}) %collective-permute-start.1) | collective-permute-done | bytes 147488 | tf_op jit(solution)/shard_map/ppermute | solution.py:422
  14.3 0.7 copy-done.2
  14.9 3.5 %pack.1 = (f32[3,10,8,128]{3,2,1,0:T(8,128)}, f32[3,10,8,128]{3,2,1,0:T(8,128)}, f32[36,8,128]{2,1,0:T(8,128)}) custom-call(f32[32,64,128]{2,1,0:T(8,128)} %right_ref.3, f32[4,64,128]{2,1,0:T(8,128)} %pad_maximum_fusion.planes_ref, f32[36,8,128]{2,1,0:T(8,128)} %copy-done, f32[36,8,128]{2,1,0:T(8,128)} %copy-done.2, f32[36,8,128]{2,1,0:T(8,128)} %copy-done.1), custom_call_target="tpu_custom_call" | custom-call | tf_op jit(solution)/shard_map/pack/pallas_call | solution.py:398
  18.4 1.8 %collective-permute-start.4 = (f32[3,10,8,128]{3,2,1,0:T(8,128)}, f32[3,10,8,128]{3,2,1,0:T(8,128)S(1)}, u32[]{:S(2)}, u32[]{:S(2)}) collective-permute-start(f32[3,10,8,128]{3,2,1,0:T(8,128)} %get-tuple-element.9.own_west_ref), channel_id=1, source_target_pairs={{1,0},{2,1},{3,2},{4,3},{5,4},{6,5},{7,6},{0,7},{9,8},{10,9},{11,1... | collective-permute-start | bytes 368648 | tf_op jit(solution)/shard_map/ppermute | solution.py:432
  20.2 1.2 %collective-permute-start.3 = (f32[3,10,8,128]{3,2,1,0:T(8,128)}, f32[3,10,8,128]{3,2,1,0:T(8,128)S(1)}, u32[]{:S(2)}, u32[]{:S(2)}) collective-permute-start(f32[3,10,8,128]{3,2,1,0:T(8,128)} %get-tuple-element.10.own_east_ref), channel_id=1, source_target_pairs={{0,1},{1,2},{2,3},{3,4},{4,5},{5,6},{6,7},{7,0},{8,9},{9,10},{10,1... | collective-permute-start | bytes 368648 | tf_op jit(solution)/shard_map/ppermute | solution.py:431
  21.4 2.8 %collective-permute-done.4.from_east_ref = f32[3,10,8,128]{3,2,1,0:T(8,128)S(1)} collective-permute-done((f32[3,10,8,128]{3,2,1,0:T(8,128)}, f32[3,10,8,128]{3,2,1,0:T(8,128)S(1)}, u32[]{:S(2)}, u32[]{:S(2)}) %collective-permute-start.4) | collective-permute-done | bytes 122912 | tf_op jit(solution)/shard_map/ppermute | solution.py:432
  24.2 0.6 copy-done.3
  24.8 0.0 copy-done.4
  24.8 25.7 %basis.1 = (f32[7,2576,128]{2,1,0:T(8,128)}, f32[64,128]{1,0:T(8,128)}, f32[8,128]{1,0:T(8,128)}) custom-call(s32[1]{0:T(128)} %bitcast.top_ref, f32[32,64,128]{2,1,0:T(8,128)} %right_ref.3, f32[4,64,128]{2,1,0:T(8,128)} %pad_maximum_fusion.planes_ref, f32[36,8,128]{2,1,0:T(8,128)} %copy-done, f32[36,8,128]{2,1,0:T(8,128)} %get-tuple-element.8.north_ref, ...), custom_call_target="tpu_custom_call" | custom-call | tf_op jit(solution)/shard_map/basis/pallas_call | solution.py:398
  50.6 0.7 broadcast_in_dim.21
  51.2 10.1 %all_to_all.10 = f32[8,8,128]{2,1,0:T(8,128)S(1)} all-to-all(f32[8,8,128]{2,1,0:T(8,128)S(1)} %broadcast_in_dim.21), channel_id=1, replica_groups=mesh['gy_0'=8,'gy_1'=4,'gx_0'=4,'gx_1'=2] {'gx_0','gx_1'}, dimensions={0} | all-to-all | bytes 65536 | tf_op jit(solution)/shard_map/all_to_all | solution.py:412
  61.5 24.3 %all_to_all.11.total_ref = f32[32,2,8,128]{3,2,1,0:T(8,128)} all-to-all(f32[32,2,8,128]{3,2,1,0:T(8,128)S(1)} %broadcast_in_dim.22), channel_id=1, replica_groups=mesh['gy_0'=8,'gy_1'=4,'gx_0'=4,'gx_1'=2] {'gy_0','gy_1'}, dimensions={0} | all-to-all | bytes 524288 | tf_op jit(solution)/shard_map/all_to_all | solution.py:412
  85.7 8.0 %finish.1 = (f32[32,64,128]{2,1,0:T(8,128)}, f32[32,64,128]{2,1,0:T(8,128)}) custom-call(f32[32,2,8,128]{3,2,1,0:T(8,128)} %all_to_all.11.total_ref, f32[7,2576,128]{2,1,0:T(8,128)} %get-tuple-element.12.basis_ref, f32[64,128]{1,0:T(8,128)} %get-tuple-element.13.diag_ref), custom_call_target="tpu_custom_call" | custom-call | tf_op jit(solution)/shard_map/finish/pallas_call | solution.py:398
  (14 shorter events, 0.1 us)
Async XLA Ops:
  3.1 7.6 %collective-permute-start = (f32[36,8,128]{2,1,0:T(8,128)S(1)}, f32[36,8,128]{2,1,0:T(8,128)S(1)}, u32[]{:S(2)}, u32[]{:S(2)}) collective-permute-start(f32[36,8,128]{2,1,0:T(8,128)S(1)} %pad_maximum_fusion.1), channel_id=1, source_target_pairs={{0,8},{8,16},{16,24},{24,32},{32,40},{40,48},{48,56},{56,64},{64,7... | collective-permute-start | bytes 442376 | tf_op jit(solution)/shard_map/ppermute | solution.py:421
  7.2 3.6 %collective-permute-start.2 = (f32[36,8,128]{2,1,0:T(8,128)S(1)}, f32[36,8,128]{2,1,0:T(8,128)S(1)}, u32[]{:S(2)}, u32[]{:S(2)}) collective-permute-start(f32[36,8,128]{2,1,0:T(8,128)S(1)} %rev.3), channel_id=1, source_target_pairs={{248,255},{249,254},{250,253},{251,252},{252,251},{253,250},{254,2... | collective-permute-start | bytes 442376 | tf_op jit(solution)/shard_map/ppermute | solution.py:424
  7.9 6.3 %collective-permute-start.1 = (f32[36,8,128]{2,1,0:T(8,128)S(1)}, f32[36,8,128]{2,1,0:T(8,128)S(1)}, u32[]{:S(2)}, u32[]{:S(2)}) collective-permute-start(f32[36,8,128]{2,1,0:T(8,128)S(1)} %pad_maximum_fusion.2), channel_id=1, source_target_pairs={{8,0},{16,8},{24,16},{32,24},{40,32},{48,40},{56,48},{64,56},{72,6... | collective-permute-start | bytes 442376 | tf_op jit(solution)/shard_map/ppermute | solution.py:422
  10.8 3.5 %copy-start.1 = (f32[36,8,128]{2,1,0:T(8,128)}, f32[36,8,128]{2,1,0:T(8,128)S(1)}, u32[]{:S(2)}) copy-start(f32[36,8,128]{2,1,0:T(8,128)S(1)} %collective-permute-done.2.fold_ref) | copy-start | bytes 442372
  10.8 3.5 %copy-start = (f32[36,8,128]{2,1,0:T(8,128)}, f32[36,8,128]{2,1,0:T(8,128)S(1)}, u32[]{:S(2)}) copy-start(f32[36,8,128]{2,1,0:T(8,128)S(1)} %collective-permute-done.south_ref) | copy-start | bytes 442372
  14.3 0.7 copy-start.2
  18.4 5.8 %collective-permute-start.4 = (f32[3,10,8,128]{3,2,1,0:T(8,128)}, f32[3,10,8,128]{3,2,1,0:T(8,128)S(1)}, u32[]{:S(2)}, u32[]{:S(2)}) collective-permute-start(f32[3,10,8,128]{3,2,1,0:T(8,128)} %get-tuple-element.9.own_west_ref), channel_id=1, source_target_pairs={{1,0},{2,1},{3,2},{4,3},{5,4},{6,5},{7,6},{0,7},{9,8},{10,9},{11,1... | collective-permute-start | bytes 368648 | tf_op jit(solution)/shard_map/ppermute | solution.py:432
  20.2 4.0 %collective-permute-start.3 = (f32[3,10,8,128]{3,2,1,0:T(8,128)}, f32[3,10,8,128]{3,2,1,0:T(8,128)S(1)}, u32[]{:S(2)}, u32[]{:S(2)}) collective-permute-start(f32[3,10,8,128]{3,2,1,0:T(8,128)} %get-tuple-element.10.own_east_ref), channel_id=1, source_target_pairs={{0,1},{1,2},{2,3},{3,4},{4,5},{5,6},{6,7},{7,0},{8,9},{9,10},{10,1... | collective-permute-start | bytes 368648 | tf_op jit(solution)/shard_map/ppermute | solution.py:431
  24.2 0.6 copy-start.3
  24.2 0.7 copy-start.4
where the time goes:
time: 94.4 us; the launch traced here: 93.7 us
  Pallas kernels  37.2 us (39%)
  blocking collectives  34.4 us (36%)
  starting transfers between devices  8.9 us (9%)
  waiting for transfers between devices  6.24 us (7%)
  local copies, waits for them, and re-layouts  3.16 us (3%)
  other arithmetic  3.13 us (3%)
    pallas_call x3, Pallas kernels, call(): pl.pallas_call(kernel, out_shape=out_shape, in_specs=in_specs or [VMEM] *...  37.2 us
    all_to_all x2, blocking collectives, from_everyone(): lax.all_to_all(jnp.broadcast_to(value[None], (peers, *value.shape)), axis...  34.4 us
    ppermute x1, starting transfers between devices, on_device(): south = lax.ppermute(last, GY, [(k, k + 1) for k in range(ny - 1)])  3.94 us
    ppermute x1, waiting for transfers between devices, on_device(): north = lax.ppermute(first, GY, [(k + 1, k) for k in range(ny - 1)])  3.47 us
    ppermute x1, waiting for transfers between devices, on_device(): lax.ppermute(own_west, GX, [((k + 1) % nx, k) for k in range(nx)])  2.77 us
    concatenate x2, other arithmetic, on_device(): jnp.concatenate([couplings, jnp.where(ocean_mask != 0, center, 0.0)[None]...  2.28 us
  transfers between devices with their start and end apart: 5, of which 2 were waited for; matrix products, arithmetic and copies ran while one was open for 2% of the time, Pallas kernels for 0%

commit v1 on v0

v1 whole, which is shorter than its diff:
```python
import jax
import jax.numpy as jnp
from jax import lax
from jax.experimental import pallas as pl
from jax.experimental.pallas import tpu as pltpu
from jax.sharding import Mesh
from jax.sharding import PartitionSpec as P

ITERS = 6
SHIFT = (0.375, 0.0, 0.375, 0.0, 0.375, 0.0)
GY = ("gy_0", "gy_1")
GX = ("gx_0", "gx_1")
ALL = GY + GX
NEAR = ("gy_0", "gx_1")
FAR = ("gy_1", "gx_0")
MEMBERS = 32
ROWS = 64
LANES = 128
HALO = 8
TILES = (ROWS + 2 * HALO) // 8
EXT = ROWS + 2 * HALO
GROUPS = MEMBERS // 4
PLANES = 4
BASIS = ITERS + 1
PAIRS = [(i, j) for i in range(ITERS) for j in range(i, BASIS)]
INTERPRET = False
F32 = jnp.float32
VMEM = pl.BlockSpec(memory_space=pltpu.VMEM)
SMEM = pl.BlockSpec(memory_space=pltpu.SMEM)
HBM = pl.BlockSpec(memory_space=pltpu.HBM)


def lanes_of():
    return lax.broadcasted_iota(jnp.int32, (8, LANES), 1)


def rolled(value, shift):
    shift %= LANES
    return value if shift == 0 else pltpu.roll(value, shift, 1)


SENT = 6
PACKED = MEMBERS * SENT + PLANES * 8


def edges_kernel(
    right_ref, couplings_ref, center_ref, mask_ref, planes_ref, last_ref, first_ref, rows_ref, center_row_ref, mask_row_ref, sems
):
    copies = [
        pltpu.make_async_copy(couplings_ref, planes_ref.at[pl.ds(0, 3)], sems.at[0]),
        pltpu.make_async_copy(center_ref, center_row_ref, sems.at[1]),
        pltpu.make_async_copy(mask_ref, mask_row_ref, sems.at[2]),
        pltpu.make_async_copy(right_ref.at[:, pl.ds(ROWS - 8, 8), :], rows_ref.at[0], sems.at[3]),
        pltpu.make_async_copy(right_ref.at[:, pl.ds(0, 8), :], rows_ref.at[1], sems.at[4]),
    ]
    for copy in copies:
        copy.start()
    for copy in copies:
        copy.wait()
    planes_ref[3] = jnp.where(mask_row_ref[...] != 0, center_row_ref[...], 0.0)
    for p in range(PLANES):
        base = MEMBERS * SENT + 8 * p
        last_ref[base : base + 8] = planes_ref[p, ROWS - 8 : ROWS]
        first_ref[base : base + 8] = planes_ref[p, 0:8]
    for m in range(MEMBERS):
        last_ref[SENT * m : SENT * m + SENT] = rows_ref[0, m, 8 - SENT : 8]
        first_ref[SENT * m : SENT * m + SENT] = rows_ref[1, m, 0:SENT]


def pack(load, store, west_ref, east_ref, tile):
    window = lanes_of() // 8
    for h in range(3):
        members = range(16 * h, 16 * h + 16) if h < 2 else range(MEMBERS, MEMBERS + PLANES)
        first = last = None
        for m in members:
            value = rolled(load(m), 32 * (m % 4))
            if m < MEMBERS:
                store(m, value)
            extra = 8 * (m // 4 % 4) if h < 2 else 0
            low, high = rolled(value, extra), rolled(value, extra + 8)
            if first is None:
                first, last = low, high
            else:
                here = window == 4 * (m % 4) + extra // 8
                first = jnp.where(here, low, first)
                last = jnp.where(here, high, last)
        west_ref[h, tile] = first
        east_ref[h, tile] = last


def pack_own_kernel(right_hbm_ref, planes_ref, turned_ref, west_ref, east_ref, right_ref, sem):
    copy = pltpu.make_async_copy(right_hbm_ref, right_ref, sem)
    copy.start()
    copy.wait()

    def own(t, _):
        at = pl.multiple_of(8 * t, 8)

        def load(m):
            return right_ref[m, pl.ds(at, 8), :] if m < MEMBERS else planes_ref[m - MEMBERS, pl.ds(at, 8), :]

        def store(m, value):
            turned_ref[m, pl.ds(at, 8), :] = value

        pack(load, store, west_ref, east_ref, t)
        return 0

    lax.fori_loop(0, ROWS // 8, own, 0)


def pack_halo_kernel(
    south_ref, north_ref, fold_ref, own_west_ref, own_east_ref, turned_ref, planes_ref, west_ref, east_ref, rows_ref
):
    for h in range(3):
        west_ref[h, 1 : TILES - 1] = own_west_ref[h]
        east_ref[h, 1 : TILES - 1] = own_east_ref[h]
    zero = jnp.zeros((8, LANES), F32)
    for m in range(MEMBERS):
        rows_ref[0, m] = zero
        rows_ref[1, m] = zero
        rows_ref[0, m, 8 - SENT : 8] = south_ref[SENT * m : SENT * m + SENT]
        back = PACKED - SENT * (m + 1)
        rows_ref[1, m, 0:SENT] = north_ref[SENT * m : SENT * m + SENT] + fold_ref[back : back + SENT]
    for p in range(PLANES):
        base = MEMBERS * SENT + 8 * p
        back = PACKED - base - 8
        planes_ref[p, 0] = south_ref[base : base + 8]
        planes_ref[p, 1] = north_ref[base : base + 8] + fold_ref[back : back + 8]
    for k, tile in ((0, 0), (1, TILES - 1)):
        def load(m, k=k):
            return rows_ref[k, m] if m < MEMBERS else planes_ref[m - MEMBERS, k]

        def store(m, value, k=k):
            turned_ref[m, k] = value

        pack(load, store, west_ref, east_ref, tile)


def basis_kernel(
    top_ref, right_ref, right_halo_ref, planes_ref, planes_halo_ref,
    own_west_ref, own_east_ref, from_west_ref, from_east_ref,
    basis_ref, diag_ref, gram_ref,
    strip_ref, plane_ref, plane_strip_ref, weight_ref, weight_strip_ref, inverse_ref, inverse_strip_ref,
    edge_ref, partial_ref,
):
    lane = lanes_of()
    spot = (lane + 7) % 32

    def main_row(member, tile):
        return 8 + member * EXT + 8 * tile

    def at8(row):
        return pl.ds(pl.multiple_of(row, 8), 8)

    zero = jnp.zeros((8, LANES), F32)
    for j in range(ITERS):
        basis_ref[j, 0:8] = zero
        basis_ref[j, 8 + MEMBERS * EXT : 16 + MEMBERS * EXT] = zero
        strip_ref[j, 0:8] = zero
        strip_ref[j, 8 + GROUPS * EXT : 16 + GROUPS * EXT] = zero

    for p in range(PLANES):
        base = 8 + p * EXT
        plane_ref[base : base + 8] = planes_halo_ref[p, 0]
        plane_ref[base + 8 : base + 8 + ROWS] = planes_ref[p]
        plane_ref[base + 8 + ROWS : base + EXT] = planes_halo_ref[p, 1]
    plane_ref[0:8] = zero
    plane_ref[8 + PLANES * EXT : 16 + PLANES * EXT] = zero
    plane_strip_ref[0:8] = zero
    plane_strip_ref[8 + PLANES * EXT : 16 + PLANES * EXT] = zero

    def joined(h, tile, at):
        out = rolled(from_west_ref[h, tile], -7 - at)
        out = jnp.where(spot < 8, out, rolled(own_west_ref[h, tile], 1 - at))
        out = jnp.where(spot < 16, out, rolled(own_east_ref[h, tile], 9 - at))
        return jnp.where(spot < 24, out, rolled(from_east_ref[h, tile], 17 - at))

    def plane_strips(t, _):
        value = joined(2, t, 0)
        for p in range(PLANES):
            one = jnp.where((lane + 7) // 32 % 4 == p, value, 0.0)
            one = one + pltpu.roll(one, 32, 1)
            one = one + pltpu.roll(one, 64, 1)
            plane_strip_ref[at8(8 + p * EXT + 8 * t), :] = one
        return 0

    lax.fori_loop(0, TILES, plane_strips, 0)

    def weights(t, ghost):
        dr = 1 if ghost else -1
        side = LANES - 1 if ghost else 1

        def row(ref, p, shift):
            return ref[pl.ds(8 + p * EXT + 8 * t + shift, 8), :]

        def beside(main, strip):
            if ghost:
                return jnp.where(lane == LANES - 1, pltpu.roll(strip, 110, 1), pltpu.roll(main, side, 1))
            return jnp.where(lane == 0, strip, pltpu.roll(main, side, 1))

        def finish(cn0, cnr, ce0, cec, cc0, ccr, ccc, ccrc, center, main):
            total = center + cn0 + cnr + ce0 + cec + cc0 + ccr + ccc + ccrc
            inv = jnp.where(center > 0.0, 1.0 / total, 0.0)
            if ghost:
                w = dict(s=cn0, n=cnr, w=ce0, e=cec, sw=cc0, nw=ccr, se=ccc, ne=ccrc)
            else:
                w = dict(n=cn0, s=cnr, e=ce0, w=cec, ne=cc0, se=ccr, nw=ccc, sw=ccrc)

            def ahead(value):
                value = pltpu.roll(value * inv, 1, 1)
                return jnp.where(lane == 0, 0.0, value) if main else value

            def behind(value):
                value = pltpu.roll(value * inv, LANES - 1, 1)
                return jnp.where(lane == LANES - 1, 0.0, value) if main else value

            return total, inv, (
                w["s"] * inv, w["n"] * inv,
                ahead(w["se"]), ahead(w["e"]), ahead(w["ne"]),
                behind(w["sw"]), behind(w["w"]), behind(w["nw"]),
            )

        strips = [row(plane_strip_ref, p, 0) for p in range(PLANES)]
        strips_r = [row(plane_strip_ref, p, dr) for p in (0, 2)]
        _, inv, ws = finish(
            strips[0], strips_r[0], strips[1], pltpu.roll(strips[1], side, 1),
            strips[2], strips_r[1], pltpu.roll(strips[2], side, 1), pltpu.roll(strips_r[1], side, 1),
            strips[3], False,
        )
        inverse_strip_ref[t] = inv
        for k in range(8):
            weight_strip_ref[t, k] = ws[k]
        mains = [row(plane_ref, p, 0) for p in range(PLANES)]
        mains_r = [row(plane_ref, p, dr) for p in (0, 2)]
        total, inv, ws = finish(
            mains[0], mains_r[0], mains[1], beside(mains[1], strips[1]),
            mains[2], mains_r[1], beside(mains[2], strips[2]), beside(mains_r[1], strips_r[1]),
            mains[3], True,
        )
        for q in range(4):
            inverse_ref[t, q] = rolled(inv, 32 * q)
            for k in range(8):
                weight_ref[t, q, k] = rolled(ws[k], 32 * q)
        return total

    weights(0, False)

    def inner_weights(t, _):
        total = weights(t, False)
        for q in range(4):
            diag_ref[q, at8(8 * (t - 1)), :] = rolled(total, 32 * q)
        return 0

    lax.fori_loop(1, TILES - 1, inner_weights, 0)

    @pl.when(top_ref[0] == 0)
    def _():
        weights(TILES - 1, False)

    @pl.when(top_ref[0] != 0)
    def _():
        weights(TILES - 1, True)

    def first(t, load):
        for q in range(4):
            inv = inverse_ref[t, q]
            for s in range(GROUPS):
                m = 4 * s + q
                basis_ref[0, at8(main_row(m, t)), :] = load(m) * inv
        inv = inverse_strip_ref[t]
        for s in range(GROUPS):
            strip_ref[0, at8(8 + s * EXT + 8 * t), :] = joined(s // 4, t, 8 * (s % 4)) * inv

    first(0, lambda m: right_halo_ref[m, 0])

    def inner_first(t, _):
        first(t, lambda m: right_ref[m, at8(8 * (t - 1)), :])
        return 0

    lax.fori_loop(1, TILES - 1, inner_first, 0)
    first(TILES - 1, lambda m: right_halo_ref[m, 1])

    def parts(ref, j, base, w):
        a = ref[j, pl.ds(base - 1, 8), :]
        b = ref[j, at8(base), :]
        c = ref[j, pl.ds(base + 1, 8), :]
        middle = w[0] * a + w[1] * c
        if SHIFT[j]:
            middle = middle - SHIFT[j] * b
        return middle, (w[2] * a + w[4] * c) + w[3] * b, (w[5] * a + w[7] * c) + w[6] * b

    one = top_ref[1]

    def staged(work):
        waiting = []
        for begin, end in work:
            waiting.append((end, begin()))
            if len(waiting) > 2:
                end, values = waiting.pop(0)
                end(values)
        for end, values in waiting:
            end(values)

    def strip_work(j, t):
        def begin():
            w = [weight_strip_ref[t, k] for k in range(8)]
            values = []
            for s in range(GROUPS):
                middle, ahead, behind = parts(strip_ref, j, 8 + s * EXT + 8 * t, w)
                edge = jnp.where(lane % 32 == 31, pltpu.roll(ahead, LANES - 18, 1), behind)
                moved = (pltpu.roll(ahead, LANES - 1, 1), pltpu.roll(behind, 1, 1)) if j + 1 < ITERS else ()
                values.append((middle, edge, moved))
            return values

        def end(values):
            for s, (middle, edge, moved) in enumerate(values):
                edge_ref[t, s] = edge
                if moved:
                    strip_ref[j + one, at8(8 + s * EXT + 8 * t), :] = middle + moved[0] + moved[1]

        return begin, end

    def main_work(j, t, q, groups):
        def begin():
            w = [weight_ref[t, q, k] for k in range(8)]
            ends = (lane == 32 * q) | (lane == (32 * q - 1) % LANES)
            values = []
            for s in groups:
                middle, ahead, behind = parts(basis_ref, j, main_row(4 * s + q, t), w)
                middle = middle + jnp.where(ends, edge_ref[t, s], 0.0)
                values.append((middle, pltpu.roll(ahead, LANES - 1, 1), pltpu.roll(behind, 1, 1)))
            return values

        def end(values):
            for s, (middle, ahead, behind) in zip(groups, values):
                basis_ref[j + one, at8(main_row(4 * s + q, t)), :] = middle + ahead + behind

        return begin, end

    for j in range(ITERS):
        low, high = (0, TILES) if j + 1 < ITERS else (1, TILES - 1)
        half = (high - low) // 2

        def strip_body(n, _, j=j, low=low, half=half):
            staged([strip_work(j, low + half * n + k) for k in range(half)])
            return 0

        def main_body(n, _, j=j, low=low):
            staged([
                main_work(j, low + 2 * n + k, q, range(g, g + 8))
                for k in range(2) for q in range(4) for g in range(0, GROUPS, 8)
            ])
            return 0

        lax.fori_loop(0, 2, strip_body, 0)
        lax.fori_loop(0, (high - low) // 2, main_body, 0)

    def products(s, _):
        for q in range(4):
            m = 4 * s + q
            sums = [None] * len(PAIRS)
            for t in range(1, TILES - 1):
                u = [basis_ref[j, at8(main_row(m, t)), :] for j in range(BASIS)]
                d = diag_ref[q, 8 * (t - 1) : 8 * t]
                scaled = [d * u[j] for j in range(ITERS)]
                for n, (i, j) in enumerate(PAIRS):
                    term = scaled[i] * u[j]
                    sums[n] = term if sums[n] is None else sums[n] + term
            for n in range(len(PAIRS)):
                partial_ref[at8((n * MEMBERS + m) * 8), :] = sums[n]
        return 0

    lax.fori_loop(0, GROUPS, products, 0)
    result = zero
    for l in range(len(PAIRS) * MEMBERS // 8):
        rows = [partial_ref[pl.ds(64 * l + k, 8, stride=8), :] for k in range(8)]
        while len(rows) > 1:
            rows = [rows[k] + rows[k + 1] for k in range(0, len(rows), 2)]
        result = jnp.where(lane == l, jnp.sum(rows[0], axis=1, keepdims=True), result)
    for n in range(gram_ref.shape[0]):
        gram_ref[n] = result


def two_sum(a, b):
    s = a + b
    t = s - a
    return s, (a - (s - t)) + (b - t)


def quick(a, b):
    s = a + b
    return s, b - (s - a)


def halves(a):
    t = 4097.0 * a
    high = t - (t - a)
    return high, a - high


def add2(a, b):
    s, e = two_sum(a[0], b[0])
    return quick(s, e + (a[1] + b[1]))


def mul2(a, b):
    p = a[0] * b[0]
    ah, al = halves(a[0])
    bh, bl = halves(b[0])
    e = ((ah * bh - p) + ah * bl + al * bh) + al * bl
    return quick(p, e + (a[0] * b[1] + a[1] * b[0]))


def neg2(a):
    return -a[0], -a[1]


def div2(a, b):
    q = a[0] / b[0]
    zero = jnp.zeros_like(q)
    rest = add2(a, neg2(mul2((q, zero), b)))
    return quick(q, rest[0] / b[0])


def sum2(terms):
    terms = list(terms)
    while len(terms) > 1:
        terms = [add2(terms[k], terms[k + 1]) if k + 1 < len(terms) else terms[k] for k in range(0, len(terms), 2)]
    return terms[0]


def finish_kernel(total_ref, basis_ref, diag_ref, solved_ref, left_ref, coeff_ref, solution_ref, residual_ref, sems):
    count = total_ref.shape[0]
    high, low = sum2([(total_ref[n, 0], total_ref[n, 1]) for n in range(count)])
    gram = {}
    for n, (i, j) in enumerate(PAIRS):
        shift = (LANES - 4 * n) % LANES
        value = (high, low) if shift == 0 else (pltpu.roll(high, shift, 1), pltpu.roll(low, shift, 1))
        gram[i, j] = gram[j, i] = value

    def scaled(value, factor):
        if factor == 1.0:
            return value
        s, e = two_sum(0.5 * value[0], 0.125 * value[0])
        return quick(s, e + factor * value[1])

    def dot(a, b):
        return sum2([mul2(x, y) for x, y in zip(a, b)])

    one = (jnp.ones((8, LANES), F32), jnp.zeros((8, LANES), F32))
    precond, direction, answer = [one], [one], []
    rz = gram[0, 0]
    for k in range(ITERS):
        image = [scaled(c, 1.0 - SHIFT[j]) for j, c in enumerate(direction)]
        image = [image[0]] + [
            add2(image[j], neg2(direction[j - 1])) for j in range(1, k + 1)
        ] + [neg2(direction[k])]
        final = k + 1 == ITERS
        row = [dot([gram[i, j] for j in range(k + 2)], image) for i in range(k + 1 if final else k + 2)]
        step_size = div2(rz, dot(direction, row))
        moved = [mul2(step_size, c) for c in direction]
        answer = [add2(a, b) for a, b in zip(answer, moved)] + moved[len(answer):]
        if not final:
            cross = dot(precond, row)
            rz_new = mul2(step_size, add2(mul2(step_size, dot(image, row)), (-2.0 * cross[0], -2.0 * cross[1])))
            rz_new = add2(rz, rz_new)
        moved = [neg2(mul2(step_size, c)) for c in image]
        precond = [add2(a, b) for a, b in zip(precond, moved)] + moved[len(precond):]
        if not final:
            ratio = div2(rz_new, rz)
            moved = [mul2(ratio, c) for c in direction]
            direction = [add2(a, b) for a, b in zip(precond, moved)] + precond[len(moved):]
            rz = rz_new

    values = [c[0] for c in answer] + [c[0] for c in precond]
    for n, value in enumerate(values):
        for l in range(MEMBERS // 8):
            coeff_ref[n, 8 * l : 8 * l + 8] = jnp.broadcast_to(value[:, l : l + 1], (8, LANES))

    def combine(s, _):
        for q in range(4):
            m = 4 * s + q
            c = [jnp.broadcast_to(coeff_ref[n, pl.ds(m, 1), :], (8, LANES)) for n in range(2 * ITERS + 1)]
            for t in range(ROWS // 8):
                at = pl.multiple_of(16 + m * EXT + 8 * t, 8)
                u = [basis_ref[j, pl.ds(at, 8), :] for j in range(BASIS)]
                solved = c[0] * u[0]
                left = c[ITERS] * u[0]
                for j in range(1, BASIS):
                    if j < ITERS:
                        solved = solved + c[j] * u[j]
                    left = left + c[ITERS + j] * u[j]
                solution_ref[m, 8 * t : 8 * t + 8] = rolled(solved, -32 * q)
                residual_ref[m, 8 * t : 8 * t + 8] = rolled(diag_ref[q, 8 * t : 8 * t + 8] * left, -32 * q)
        for copy in copies(s):
            copy.start()
        return 0

    def copies(s):
        members = pl.ds(4 * s, 4)
        return [
            pltpu.make_async_copy(source.at[members], target.at[members], sems.at[n, s])
            for n, (source, target) in enumerate(((solution_ref, solved_ref), (residual_ref, left_ref)))
        ]

    lax.fori_loop(0, GROUPS, combine, 0)
    for s in range(GROUPS):
        for copy in copies(s):
            copy.wait()


def shape(*dims):
    return jax.ShapeDtypeStruct(dims, F32)


def call(kernel, inputs, out_shape, scratch=(), name=None, in_specs=None, out_specs=None):
    return pl.pallas_call(
        kernel,
        out_shape=out_shape,
        in_specs=in_specs or [VMEM] * len(inputs),
        out_specs=out_specs or [VMEM] * len(out_shape),
        scratch_shapes=list(scratch),
        interpret=INTERPRET,
        name=name,
        compiler_params=pltpu.CompilerParams(vmem_limit_bytes=28 * 1024 * 1024),
    )(*inputs)


def on_device(right_side, couplings, center, ocean_mask):
    ny, nx = lax.axis_size(GY), lax.axis_size(GX)
    top = jnp.stack([(lax.axis_index(GY) == ny - 1).astype(jnp.int32), jnp.int32(1)])
    sent = shape(PACKED, LANES)
    right_side, couplings, center, ocean_mask = (
        pltpu.with_memory_space_constraint(a, pltpu.HBM) for a in (right_side, couplings, center, ocean_mask)
    )
    planes, last, first = call(
        edges_kernel, (right_side, couplings, center, ocean_mask), (shape(PLANES, ROWS, LANES), sent, sent),
        scratch=(
            pltpu.VMEM((2, MEMBERS, 8, LANES), F32),
            pltpu.VMEM((ROWS, LANES), F32),
            pltpu.VMEM((ROWS, LANES), jnp.int32),
            pltpu.SemaphoreType.DMA((5,)),
        ),
        name="edges",
        in_specs=[HBM] * 4,
    )
    with jax.named_scope("south"):
        south = lax.ppermute(last, GY, [(k, k + 1) for k in range(ny - 1)])
    with jax.named_scope("north"):
        north = lax.ppermute(first, GY, [(k + 1, k) for k in range(ny - 1)])
    row = (ny - 1) * nx
    turned_last = last[::-1, ::-1]
    with jax.named_scope("fold"):
        fold = lax.ppermute(turned_last, ALL, [(row + k, row + nx - 1 - k) for k in range(nx)])

    inner = shape(3, TILES - 2, 8, LANES)
    turned, inner_west, inner_east = call(
        pack_own_kernel, (right_side, planes), (shape(MEMBERS, ROWS, LANES), inner, inner), name="pack_own",
        scratch=(pltpu.VMEM((MEMBERS, ROWS, LANES), F32), pltpu.SemaphoreType.DMA),
        in_specs=[HBM, VMEM],
    )
    packed = shape(3, TILES, 8, LANES)
    turned_halo, planes_halo, own_west, own_east = call(
        pack_halo_kernel,
        (south, north, fold, inner_west, inner_east),
        (shape(MEMBERS, 2, 8, LANES), shape(PLANES, 2, 8, LANES), packed, packed),
        scratch=(pltpu.VMEM((2, MEMBERS, 8, LANES), F32),),
        name="pack_halo",
    )
    from_west = lax.ppermute(own_east, GX, [(k, (k + 1) % nx) for k in range(nx)])
    from_east = lax.ppermute(own_west, GX, [((k + 1) % nx, k) for k in range(nx)])

    near, far = lax.axis_size(NEAR), lax.axis_size(FAR)
    basis, diag, gram = call(
        basis_kernel,
        (top, turned, turned_halo, planes, planes_halo, own_west, own_east, from_west, from_east),
        (shape(BASIS, 16 + MEMBERS * EXT, LANES), shape(4, ROWS, LANES), shape(near, 8, LANES)),
        scratch=(
            pltpu.VMEM((ITERS, 16 + GROUPS * EXT, LANES), F32),
            pltpu.VMEM((16 + PLANES * EXT, LANES), F32),
            pltpu.VMEM((16 + PLANES * EXT, LANES), F32),
            pltpu.VMEM((TILES, 4, 8, 8, LANES), F32),
            pltpu.VMEM((TILES, 8, 8, LANES), F32),
            pltpu.VMEM((TILES, 4, 8, LANES), F32),
            pltpu.VMEM((TILES, 8, LANES), F32),
            pltpu.VMEM((TILES, GROUPS, 8, LANES), F32),
            pltpu.VMEM((len(PAIRS) * MEMBERS * 8, LANES), F32),
        ),
        name="basis",
        in_specs=[SMEM] + [VMEM] * 8,
    )
    parts = lax.all_to_all(gram, NEAR, 0, 0, tiled=True)
    zero = jnp.zeros((8, LANES), F32)
    mine = jnp.stack(sum2([(parts[k], zero) for k in range(near)]))
    total = lax.all_to_all(jnp.broadcast_to(mine[None], (far, *mine.shape)), FAR, 0, 0, tiled=True)
    return tuple(call(
        finish_kernel,
        (total, basis, diag),
        (shape(MEMBERS, ROWS, LANES), shape(MEMBERS, ROWS, LANES)),
        scratch=(
            pltpu.VMEM((2 * ITERS + 1, MEMBERS, LANES), F32),
            pltpu.VMEM((MEMBERS, ROWS, LANES), F32),
            pltpu.VMEM((MEMBERS, ROWS, LANES), F32),
            pltpu.SemaphoreType.DMA((2, GROUPS)),
        ),
        name="finish",
        out_specs=[HBM, HBM],
    ))


def solution(mesh):
    split = Mesh(mesh.devices.reshape(8, 4, 4, 2), ("gy_0", "gy_1", "gx_0", "gx_1"))
    placed = (P(None, GY, GX), P(None, GY, GX), P(GY, GX), P(GY, GX))
    return jax.shard_map(
        on_device,
        mesh=split,
        in_specs=placed,
        out_specs=(P(None, GY, GX), P(None, GY, GX)),
        check_vma=False,
    )
```

time: 94.4 us -> 75.6 us (0.80)
  Pallas kernels: 37.2 us -> 28.7 us
  waiting for transfers between devices: 6.24 us -> 1.97 us
  other arithmetic: 3.13 us -> 0.14 us
  local copies, waits for them, and re-layouts: 3.16 us -> 0.38 us
    pallas_call x3 -> x5, Pallas kernels: 37.2 us -> 28.7 us  [call(): pl.pallas_call(kernel, out_shape=out_shape, in_specs=in_specs or [VMEM] *...]
    ppermute x1, waiting for transfers between devices: 3.47 us -> 0.01 us  [on_device(): north = lax.ppermute(first, GY, [(k + 1, k) for k in range(ny - 1)])]
    concatenate x4 -> x0, other arithmetic: 2.31 us -> none  [the longest x2 2.28 us: on_device(): jnp.concatenate([couplings, jnp.where(ocean_mask != 0, center, 0.0)[None]...]
    ppermute x1, starting transfers between devices: 1.81 us -> 3.2 us  [on_device(): lax.ppermute(own_west, GX, [((k + 1) % nx, k) for k in range(nx)])]
    unnamed x10 -> x0, local copies, waits for them, and re-layouts: 1.36 us -> none
    ppermute x1, starting transfers between devices: 1.18 us -> 0.01 us  [on_device(): lax.ppermute(own_east, GX, [(k, (k + 1) % nx) for k in range(nx)])]
    slice x1 -> x0, local copies, waits for them, and re-layouts: 0.99 us -> none  [on_device(): first = jnp.concatenate([right_side[:, :HALO], planes[:, :HALO]], axis=0)]
  transfers between devices with their start and end apart: 5 -> 5, of which waited for: 2 -> 1; matrix products, arithmetic and copies ran while one was open for 2% -> 0% of each run, Pallas kernels for 0% -> 4%
where the time goes in v1:
time: 75.6 us; the launch traced here: 75.4 us
  blocking collectives  33.7 us (45%)
  Pallas kernels  28.7 us (38%)
  starting transfers between devices  9.73 us (13%)
  waiting for transfers between devices  1.97 us (3%)
    pallas_call x5, Pallas kernels, call(): pl.pallas_call(kernel, out_shape=out_shape, in_specs=in_specs or [VMEM] *...  28.7 us
    all_to_all x1, blocking collectives, on_device(): parts = lax.all_to_all(gram, NEAR, 0, 0, tiled=True)  24.4 us
    all_to_all x1, blocking collectives, on_device(): lax.all_to_all(jnp.broadcast_to(mine[None], (far, *mine.shape)), FAR, 0,...  9.34 us
    ppermute x1, starting transfers between devices, on_device(): south = lax.ppermute(last, GY, [(k, k + 1) for k in range(ny - 1)])  4.57 us
    ppermute x1, starting transfers between devices, on_device(): lax.ppermute(own_west, GX, [((k + 1) % nx, k) for k in range(nx)])  3.2 us
    ppermute x1, waiting for transfers between devices, on_device(): lax.ppermute(own_west, GX, [((k + 1) % nx, k) for k in range(nx)])  1.96 us
  transfers between devices with their start and end apart: 5, of which 1 were waited for; matrix products, arithmetic and copies ran while one was open for 0% of the time, Pallas kernels for 4%

profile of v1, /device:TPU:1, one launch (start us, length us, event | category | flops | bytes accessed | tf_op | source)
XLA Modules:
  0.0 75.4 jit_solution(10934050380347014403)
XLA Ops:
  0.6 1.1 %edges.1 = (f32[4,64,128]{2,1,0:T(8,128)S(1)}, f32[224,128]{1,0:T(8,128)S(1)}, f32[224,128]{1,0:T(8,128)S(1)}) custom-call(f32[32,64,128]{2,1,0:T(8,128)} %right_hbm_ref.1, f32[3,64,128]{2,1,0:T(8,128)} %couplings_ref.1, f32[64,128]{1,0:T(8,128)} %center_ref.1, s32[64,128]{1,0:T(8,128)} %mask_ref.1), custom_call_target="tpu_custom_call" | custom-call | tf_op jit(solution)/shard_map/edges/pallas_call | solution.py:517
  1.8 0.4 rev.3
  2.1 0.7 collective-permute-start.2
  2.8 1.3 %collective-permute-start.1 = (f32[224,128]{1,0:T(8,128)S(1)}, f32[224,128]{1,0:T(8,128)S(1)}, u32[]{:S(2)}, u32[]{:S(2)}) collective-permute-start(f32[224,128]{1,0:T(8,128)S(1)} %get-tuple-element.18), channel_id=1, source_target_pairs={{8,0},{16,8},{24,16},{32,24},{40,32},{48,40},{56,48},{64,56},{72,6... | collective-permute-start | bytes 344072 | tf_op jit(solution)/shard_map/north/ppermute | solution.py:550
  4.1 4.6 %collective-permute-start = (f32[224,128]{1,0:T(8,128)S(1)}, f32[224,128]{1,0:T(8,128)S(1)}, u32[]{:S(2)}, u32[]{:S(2)}) collective-permute-start(f32[224,128]{1,0:T(8,128)S(1)} %get-tuple-element.17), channel_id=1, source_target_pairs={{0,8},{8,16},{16,24},{24,32},{32,40},{40,48},{48,56},{56,64},{64,7... | collective-permute-start | bytes 344072 | tf_op jit(solution)/shard_map/south/ppermute | solution.py:548
  8.7 2.8 %pack_own.1 = (f32[32,64,128]{2,1,0:T(8,128)S(1)}, f32[3,8,8,128]{3,2,1,0:T(8,128)S(1)}, f32[3,8,8,128]{3,2,1,0:T(8,128)S(1)}) custom-call(f32[32,64,128]{2,1,0:T(8,128)} %right_hbm_ref.1, f32[4,64,128]{2,1,0:T(8,128)S(1)} %get-tuple-element.15.planes_ref), custom_call_target="tpu_custom_call" | custom-call | tf_op jit(solution)/shard_map/pack_own/pallas_call | solution.py:517
  11.5 0.0 collective-permute-done.2.fold_ref
  11.5 0.0 collective-permute-done.1.north_ref
  11.5 0.0 collective-permute-done.south_ref
  11.5 0.8 %pack_halo.1 = (f32[32,2,8,128]{3,2,1,0:T(8,128)S(1)}, f32[4,2,8,128]{3,2,1,0:T(8,128)S(1)}, f32[3,10,8,128]{3,2,1,0:T(8,128)S(1)}, f32[3,10,8,128]{3,2,1,0:T(8,128)S(1)}) custom-call(f32[224,128]{1,0:T(8,128)S(1)} %collective-permute-done.south_ref, f32[224,128]{1,0:T(8,128)S(1)} %collective-permute-done.1.north_ref, ...), custom_call_target="tpu_custom_call" | custom-call | tf_op jit(solution)/shard_map/pack_halo/pallas_call | solution.py:517
  12.3 3.2 %collective-permute-start.4 = (f32[3,10,8,128]{3,2,1,0:T(8,128)S(1)}, f32[3,10,8,128]{3,2,1,0:T(8,128)S(1)}, u32[]{:S(2)}, u32[]{:S(2)}) collective-permute-start(f32[3,10,8,128]{3,2,1,0:T(8,128)S(1)} %get-tuple-element.23.own_west_ref), channel_id=1, source_target_pairs={{1,0},{2,1},{3,2},{4,3},{5,4},{6,5},{7,6},{0,7},{9,8},{10,9},{11,1... | collective-permute-start | bytes 368648 | tf_op jit(solution)/shard_map/ppermute | solution.py:571
  15.5 0.0 collective-permute-start.3
  15.5 0.1 add_convert_fusion.top_ref
  15.6 2.0 %collective-permute-done.4.from_east_ref = f32[3,10,8,128]{3,2,1,0:T(8,128)S(1)} collective-permute-done((f32[3,10,8,128]{3,2,1,0:T(8,128)S(1)}, f32[3,10,8,128]{3,2,1,0:T(8,128)S(1)}, u32[]{:S(2)}, u32[]{:S(2)}) %collective-permute-start.4) | collective-permute-done | bytes 122912 | tf_op jit(solution)/shard_map/ppermute | solution.py:571
  17.5 0.0 collective-permute-done.3.from_west_ref
  17.5 20.3 %basis.1 = (f32[7,2576,128]{2,1,0:T(8,128)S(1)}, f32[4,64,128]{2,1,0:T(8,128)S(1)}, f32[16,8,128]{2,1,0:T(8,128)S(1)}) custom-call(s32[2]{0:T(128)S(1)} %add_convert_fusion.top_ref, f32[32,64,128]{2,1,0:T(8,128)S(1)} %get-tuple-element.16.right_ref, f32[32,2,8,128]{3,2,1,0:T(8,128)S(1)} %get-tuple-element.21.right_halo_ref, ...), custom_call_target="tpu_custom_call" | custom-call | tf_op jit(solution)/shard_map/basis/pallas_call | solution.py:517
  37.8 24.4 %all_to_all.10 = f32[16,8,128]{2,1,0:T(8,128)S(1)} all-to-all(f32[16,8,128]{2,1,0:T(8,128)S(1)} %get-tuple-element.25), channel_id=1, replica_groups=mesh['gy_0'=8,'gy_1'=4,'gx_0'=4,'gx_1'=2] {'gy_0','gx_1'}, dimensions={0} | all-to-all | bytes 131072 | tf_op jit(solution)/shard_map/all_to_all | solution.py:592
  62.3 9.3 %all_to_all.11.total_ref = f32[16,2,8,128]{3,2,1,0:T(8,128)S(1)} all-to-all(f32[16,2,8,128]{3,2,1,0:T(8,128)S(1)} %broadcast_in_dim.2), channel_id=1, replica_groups=mesh['gy_0'=8,'gy_1'=4,'gx_0'=4,'gx_1'=2] {'gy_1','gx_0'}, dimensions={0} | all-to-all | bytes 262144 | tf_op jit(solution)/shard_map/all_to_all | solution.py:595
  71.7 3.7 %finish.1 = (f32[32,64,128]{2,1,0:T(8,128)}, f32[32,64,128]{2,1,0:T(8,128)}) custom-call(f32[16,2,8,128]{3,2,1,0:T(8,128)S(1)} %all_to_all.11.total_ref, f32[7,2576,128]{2,1,0:T(8,128)S(1)} %get-tuple-element.26.basis_ref, f32[4,64,128]{2,1,0:T(8,128)S(1)} %get-tuple-element.27.diag_ref), custom_call_target="tpu_custom_call" | custom-call | tf_op jit(solution)/shard_map/finish/pallas_call | solution.py:517
  (6 shorter events, 0.1 us)
Async XLA Ops:
  2.1 9.4 %collective-permute-start.2 = (f32[224,128]{1,0:T(8,128)S(1)}, f32[224,128]{1,0:T(8,128)S(1)}, u32[]{:S(2)}, u32[]{:S(2)}) collective-permute-start(f32[224,128]{1,0:T(8,128)S(1)} %rev.3), channel_id=1, source_target_pairs={{248,255},{249,254},{250,253},{251,252},{252,251},{253,250},{254,2... | collective-permute-start | bytes 344072 | tf_op jit(solution)/shard_map/fold/ppermute | solution.py:554
  2.8 8.7 %collective-permute-start.1 = (f32[224,128]{1,0:T(8,128)S(1)}, f32[224,128]{1,0:T(8,128)S(1)}, u32[]{:S(2)}, u32[]{:S(2)}) collective-permute-start(f32[224,128]{1,0:T(8,128)S(1)} %get-tuple-element.18), channel_id=1, source_target_pairs={{8,0},{16,8},{24,16},{32,24},{40,32},{48,40},{56,48},{64,56},{72,6... | collective-permute-start | bytes 344072 | tf_op jit(solution)/shard_map/north/ppermute | solution.py:550
  4.1 7.4 %collective-permute-start = (f32[224,128]{1,0:T(8,128)S(1)}, f32[224,128]{1,0:T(8,128)S(1)}, u32[]{:S(2)}, u32[]{:S(2)}) collective-permute-start(f32[224,128]{1,0:T(8,128)S(1)} %get-tuple-element.17), channel_id=1, source_target_pairs={{0,8},{8,16},{16,24},{24,32},{32,40},{40,48},{48,56},{56,64},{64,7... | collective-permute-start | bytes 344072 | tf_op jit(solution)/shard_map/south/ppermute | solution.py:548
  12.3 5.2 %collective-permute-start.4 = (f32[3,10,8,128]{3,2,1,0:T(8,128)S(1)}, f32[3,10,8,128]{3,2,1,0:T(8,128)S(1)}, u32[]{:S(2)}, u32[]{:S(2)}) collective-permute-start(f32[3,10,8,128]{3,2,1,0:T(8,128)S(1)} %get-tuple-element.23.own_west_ref), channel_id=1, source_target_pairs={{1,0},{2,1},{3,2},{4,3},{5,4},{6,5},{7,6},{0,7},{9,8},{10,9},{11,1... | collective-permute-start | bytes 368648 | tf_op jit(solution)/shard_map/ppermute | solution.py:571
  15.5 2.0 %collective-permute-start.3 = (f32[3,10,8,128]{3,2,1,0:T(8,128)S(1)}, f32[3,10,8,128]{3,2,1,0:T(8,128)S(1)}, u32[]{:S(2)}, u32[]{:S(2)}) collective-permute-start(f32[3,10,8,128]{3,2,1,0:T(8,128)S(1)} %get-tuple-element.24.own_east_ref), channel_id=1, source_target_pairs={{0,1},{1,2},{2,3},{3,4},{4,5},{5,6},{6,7},{7,0},{8,9},{9,10},{10,1... | collective-permute-start | bytes 368648 | tf_op jit(solution)/shard_map/ppermute | solution.py:570

commit v2 on v1

--- a/solution.py
+++ b/solution.py
@@ -184,7 +184,7 @@
             plane_strip_ref[at8(8 + p * EXT + 8 * t), :] = one
         return 0
 
-    lax.fori_loop(0, TILES, plane_strips, 0)
+    lax.fori_loop(0, TILES, plane_strips, 0, unroll=True)
 
     def weights(t, ghost):
         dr = 1 if ghost else -1
@@ -251,7 +251,7 @@
             diag_ref[q, at8(8 * (t - 1)), :] = rolled(total, 32 * q)
         return 0
 
-    lax.fori_loop(1, TILES - 1, inner_weights, 0)
+    lax.fori_loop(1, TILES - 1, inner_weights, 0, unroll=4)
 
     @pl.when(top_ref[0] == 0)
     def _():
@@ -277,7 +277,7 @@
         first(t, lambda m: right_ref[m, at8(8 * (t - 1)), :])
         return 0
 
-    lax.fori_loop(1, TILES - 1, inner_first, 0)
+    lax.fori_loop(1, TILES - 1, inner_first, 0, unroll=4)
     first(TILES - 1, lambda m: right_halo_ref[m, 1])
 
     def parts(ref, j, base, w):
@@ -289,16 +289,9 @@
             middle = middle - SHIFT[j] * b
         return middle, (w[2] * a + w[4] * c) + w[3] * b, (w[5] * a + w[7] * c) + w[6] * b
 
-    one = top_ref[1]
-
     def staged(work):
-        waiting = []
-        for begin, end in work:
-            waiting.append((end, begin()))
-            if len(waiting) > 2:
-                end, values = waiting.pop(0)
-                end(values)
-        for end, values in waiting:
+        begun = [(end, begin()) for begin, end in work]
+        for end, values in begun:
             end(values)
 
     def strip_work(j, t):
@@ -316,7 +309,7 @@
             for s, (middle, edge, moved) in enumerate(values):
                 edge_ref[t, s] = edge
                 if moved:
-                    strip_ref[j + one, at8(8 + s * EXT + 8 * t), :] = middle + moved[0] + moved[1]
+                    strip_ref[j + 1, at8(8 + s * EXT + 8 * t), :] = middle + moved[0] + moved[1]
 
         return begin, end
 
@@ -333,7 +326,7 @@
 
         def end(values):
             for s, (middle, ahead, behind) in zip(groups, values):
-                basis_ref[j + one, at8(main_row(4 * s + q, t)), :] = middle + ahead + behind
+                basis_ref[j + 1, at8(main_row(4 * s + q, t)), :] = middle + ahead + behind
 
         return begin, end
 
@@ -345,15 +338,12 @@
             staged([strip_work(j, low + half * n + k) for k in range(half)])
             return 0
 
-        def main_body(n, _, j=j, low=low):
-            staged([
-                main_work(j, low + 2 * n + k, q, range(g, g + 8))
-                for k in range(2) for q in range(4) for g in range(0, GROUPS, 8)
-            ])
+        def main_body(n, _, j=j, low=low, half=half):
+            staged([main_work(j, low + half * n + k, q, range(GROUPS)) for k in range(half) for q in range(4)])
             return 0
 
         lax.fori_loop(0, 2, strip_body, 0)
-        lax.fori_loop(0, (high - low) // 2, main_body, 0)
+        lax.fori_loop(0, 2, main_body, 0)
 
     def products(s, _):
         for q in range(4):
@@ -503,7 +493,7 @@
             for n, (source, target) in enumerate(((solution_ref, solved_ref), (residual_ref, left_ref)))
         ]
 
-    lax.fori_loop(0, GROUPS, combine, 0)
+    lax.fori_loop(0, GROUPS, combine, 0, unroll=2)
     for s in range(GROUPS):
         for copy in copies(s):
             copy.wait()
@@ -528,7 +518,7 @@
 
 def on_device(right_side, couplings, center, ocean_mask):
     ny, nx = lax.axis_size(GY), lax.axis_size(GX)
-    top = jnp.stack([(lax.axis_index(GY) == ny - 1).astype(jnp.int32), jnp.int32(1)])
+    top = (lax.axis_index(GY) == ny - 1).astype(jnp.int32).reshape(1)
     sent = shape(PACKED, LANES)
     right_side, couplings, center, ocean_mask = (
         pltpu.with_memory_space_constraint(a, pltpu.HBM) for a in (right_side, couplings, center, ocean_mask)

time: 75.6 us -> 67.4 us (0.89)
  Pallas kernels: 28.7 us -> 20.4 us
    pallas_call x5, Pallas kernels: 28.7 us -> 20.4 us  [call(): pl.pallas_call(kernel, out_shape=out_shape, in_specs=in_specs or [VMEM] *...]
where the time goes in v2:
time: 67.4 us; the launch traced here: 67.1 us
  blocking collectives  33.7 us (50%)
  Pallas kernels  20.4 us (30%)
  starting transfers between devices  9.73 us (14%)
  waiting for transfers between devices  2.05 us (3%)
  between operations  0.75 us (1%)
    all_to_all x1, blocking collectives, on_device(): parts = lax.all_to_all(gram, NEAR, 0, 0, tiled=True)  24.4 us
    pallas_call x5, Pallas kernels, call(): pl.pallas_call(kernel, out_shape=out_shape, in_specs=in_specs or [VMEM] *...  20.4 us
    all_to_all x1, blocking collectives, on_device(): lax.all_to_all(jnp.broadcast_to(mine[None], (far, *mine.shape)), FAR, 0,...  9.34 us
    ppermute x1, starting transfers between devices, on_device(): south = lax.ppermute(last, GY, [(k, k + 1) for k in range(ny - 1)])  4.57 us
    ppermute x1, starting transfers between devices, on_device(): lax.ppermute(own_west, GX, [((k + 1) % nx, k) for k in range(nx)])  3.2 us
    ppermute x1, waiting for transfers between devices, on_device(): lax.ppermute(own_west, GX, [((k + 1) % nx, k) for k in range(nx)])  2.04 us
  transfers between devices with their start and end apart: 5, of which 1 were waited for; matrix products, arithmetic and copies ran while one was open for 0% of the time, Pallas kernels for 4%

profile of v2, /device:TPU:1, one launch (start us, length us, event | category | flops | bytes accessed | tf_op | source)
XLA Modules:
  0.0 67.1 jit_solution(6340449174931459735)
XLA Ops:
  0.6 1.1 %edges.1 = (f32[4,64,128]{2,1,0:T(8,128)S(1)}, f32[224,128]{1,0:T(8,128)S(1)}, f32[224,128]{1,0:T(8,128)S(1)}) custom-call(f32[32,64,128]{2,1,0:T(8,128)} %right_hbm_ref.1, f32[3,64,128]{2,1,0:T(8,128)} %couplings_ref.1, f32[64,128]{1,0:T(8,128)} %center_ref.1, s32[64,128]{1,0:T(8,128)} %mask_ref.1), custom_call_target="tpu_custom_call" | custom-call | tf_op jit(solution)/shard_map/edges/pallas_call | solution.py:507
  1.8 0.4 rev.3
  2.1 0.7 collective-permute-start.2
  2.8 1.3 %collective-permute-start.1 = (f32[224,128]{1,0:T(8,128)S(1)}, f32[224,128]{1,0:T(8,128)S(1)}, u32[]{:S(2)}, u32[]{:S(2)}) collective-permute-start(f32[224,128]{1,0:T(8,128)S(1)} %get-tuple-element.18), channel_id=1, source_target_pairs={{8,0},{16,8},{24,16},{32,24},{40,32},{48,40},{56,48},{64,56},{72,6... | collective-permute-start | bytes 344072 | tf_op jit(solution)/shard_map/north/ppermute | solution.py:540
  4.1 4.6 %collective-permute-start = (f32[224,128]{1,0:T(8,128)S(1)}, f32[224,128]{1,0:T(8,128)S(1)}, u32[]{:S(2)}, u32[]{:S(2)}) collective-permute-start(f32[224,128]{1,0:T(8,128)S(1)} %get-tuple-element.17), channel_id=1, source_target_pairs={{0,8},{8,16},{16,24},{24,32},{32,40},{40,48},{48,56},{56,64},{64,7... | collective-permute-start | bytes 344072 | tf_op jit(solution)/shard_map/south/ppermute | solution.py:538
  8.7 2.8 %pack_own.1 = (f32[32,64,128]{2,1,0:T(8,128)S(1)}, f32[3,8,8,128]{3,2,1,0:T(8,128)S(1)}, f32[3,8,8,128]{3,2,1,0:T(8,128)S(1)}) custom-call(f32[32,64,128]{2,1,0:T(8,128)} %right_hbm_ref.1, f32[4,64,128]{2,1,0:T(8,128)S(1)} %get-tuple-element.15.planes_ref), custom_call_target="tpu_custom_call" | custom-call | tf_op jit(solution)/shard_map/pack_own/pallas_call | solution.py:507
  11.5 0.0 collective-permute-done.2.fold_ref
  11.5 0.0 collective-permute-done.1.north_ref
  11.5 0.0 collective-permute-done.south_ref
  11.5 0.8 %pack_halo.1 = (f32[32,2,8,128]{3,2,1,0:T(8,128)S(1)}, f32[4,2,8,128]{3,2,1,0:T(8,128)S(1)}, f32[3,10,8,128]{3,2,1,0:T(8,128)S(1)}, f32[3,10,8,128]{3,2,1,0:T(8,128)S(1)}) custom-call(f32[224,128]{1,0:T(8,128)S(1)} %collective-permute-done.south_ref, f32[224,128]{1,0:T(8,128)S(1)} %collective-permute-done.1.north_ref, ...), custom_call_target="tpu_custom_call" | custom-call | tf_op jit(solution)/shard_map/pack_halo/pallas_call | solution.py:507
  12.3 3.2 %collective-permute-start.4 = (f32[3,10,8,128]{3,2,1,0:T(8,128)S(1)}, f32[3,10,8,128]{3,2,1,0:T(8,128)S(1)}, u32[]{:S(2)}, u32[]{:S(2)}) collective-permute-start(f32[3,10,8,128]{3,2,1,0:T(8,128)S(1)} %get-tuple-element.23.own_west_ref), channel_id=1, source_target_pairs={{1,0},{2,1},{3,2},{4,3},{5,4},{6,5},{7,6},{0,7},{9,8},{10,9},{11,1... | collective-permute-start | bytes 368648 | tf_op jit(solution)/shard_map/ppermute | solution.py:561
  15.5 0.0 collective-permute-start.3
  15.5 2.0 %collective-permute-done.4.from_east_ref = f32[3,10,8,128]{3,2,1,0:T(8,128)S(1)} collective-permute-done((f32[3,10,8,128]{3,2,1,0:T(8,128)S(1)}, f32[3,10,8,128]{3,2,1,0:T(8,128)S(1)}, u32[]{:S(2)}, u32[]{:S(2)}) %collective-permute-start.4) | collective-permute-done | bytes 122912 | tf_op jit(solution)/shard_map/ppermute | solution.py:561
  17.5 0.0 collective-permute-done.3.from_west_ref
  17.5 12.3 %basis.1 = (f32[7,2576,128]{2,1,0:T(8,128)S(1)}, f32[4,64,128]{2,1,0:T(8,128)S(1)}, f32[16,8,128]{2,1,0:T(8,128)S(1)}) custom-call(s32[1]{0:T(128)} %bitcast.top_ref, f32[32,64,128]{2,1,0:T(8,128)S(1)} %get-tuple-element.16.right_ref, f32[32,2,8,128]{3,2,1,0:T(8,128)S(1)} %get-tuple-element.21.right_halo_ref, ...), custom_call_target="tpu_custom_call" | custom-call | tf_op jit(solution)/shard_map/basis/pallas_call | solution.py:507
  29.8 24.4 %all_to_all.10 = f32[16,8,128]{2,1,0:T(8,128)S(1)} all-to-all(f32[16,8,128]{2,1,0:T(8,128)S(1)} %get-tuple-element.25), channel_id=1, replica_groups=mesh['gy_0'=8,'gy_1'=4,'gx_0'=4,'gx_1'=2] {'gy_0','gx_1'}, dimensions={0} | all-to-all | bytes 131072 | tf_op jit(solution)/shard_map/all_to_all | solution.py:582
  54.3 9.3 %all_to_all.11.total_ref = f32[16,2,8,128]{3,2,1,0:T(8,128)S(1)} all-to-all(f32[16,2,8,128]{3,2,1,0:T(8,128)S(1)} %broadcast_in_dim.2), channel_id=1, replica_groups=mesh['gy_0'=8,'gy_1'=4,'gx_0'=4,'gx_1'=2] {'gy_1','gx_0'}, dimensions={0} | all-to-all | bytes 262144 | tf_op jit(solution)/shard_map/all_to_all | solution.py:585
  63.6 3.5 %finish.1 = (f32[32,64,128]{2,1,0:T(8,128)}, f32[32,64,128]{2,1,0:T(8,128)}) custom-call(f32[16,2,8,128]{3,2,1,0:T(8,128)S(1)} %all_to_all.11.total_ref, f32[7,2576,128]{2,1,0:T(8,128)S(1)} %get-tuple-element.26.basis_ref, f32[4,64,128]{2,1,0:T(8,128)S(1)} %get-tuple-element.27.diag_ref), custom_call_target="tpu_custom_call" | custom-call | tf_op jit(solution)/shard_map/finish/pallas_call | solution.py:507
  (6 shorter events, 0.1 us)
Async XLA Ops:
  2.1 9.4 %collective-permute-start.2 = (f32[224,128]{1,0:T(8,128)S(1)}, f32[224,128]{1,0:T(8,128)S(1)}, u32[]{:S(2)}, u32[]{:S(2)}) collective-permute-start(f32[224,128]{1,0:T(8,128)S(1)} %rev.3), channel_id=1, source_target_pairs={{248,255},{249,254},{250,253},{251,252},{252,251},{253,250},{254,2... | collective-permute-start | bytes 344072 | tf_op jit(solution)/shard_map/fold/ppermute | solution.py:544
  2.8 8.7 %collective-permute-start.1 = (f32[224,128]{1,0:T(8,128)S(1)}, f32[224,128]{1,0:T(8,128)S(1)}, u32[]{:S(2)}, u32[]{:S(2)}) collective-permute-start(f32[224,128]{1,0:T(8,128)S(1)} %get-tuple-element.18), channel_id=1, source_target_pairs={{8,0},{16,8},{24,16},{32,24},{40,32},{48,40},{56,48},{64,56},{72,6... | collective-permute-start | bytes 344072 | tf_op jit(solution)/shard_map/north/ppermute | solution.py:540
  4.1 7.4 %collective-permute-start = (f32[224,128]{1,0:T(8,128)S(1)}, f32[224,128]{1,0:T(8,128)S(1)}, u32[]{:S(2)}, u32[]{:S(2)}) collective-permute-start(f32[224,128]{1,0:T(8,128)S(1)} %get-tuple-element.17), channel_id=1, source_target_pairs={{0,8},{8,16},{16,24},{24,32},{32,40},{40,48},{48,56},{56,64},{64,7... | collective-permute-start | bytes 344072 | tf_op jit(solution)/shard_map/south/ppermute | solution.py:538
  12.3 5.2 %collective-permute-start.4 = (f32[3,10,8,128]{3,2,1,0:T(8,128)S(1)}, f32[3,10,8,128]{3,2,1,0:T(8,128)S(1)}, u32[]{:S(2)}, u32[]{:S(2)}) collective-permute-start(f32[3,10,8,128]{3,2,1,0:T(8,128)S(1)} %get-tuple-element.23.own_west_ref), channel_id=1, source_target_pairs={{1,0},{2,1},{3,2},{4,3},{5,4},{6,5},{7,6},{0,7},{9,8},{10,9},{11,1... | collective-permute-start | bytes 368648 | tf_op jit(solution)/shard_map/ppermute | solution.py:561
  15.5 2.0 %collective-permute-start.3 = (f32[3,10,8,128]{3,2,1,0:T(8,128)S(1)}, f32[3,10,8,128]{3,2,1,0:T(8,128)S(1)}, u32[]{:S(2)}, u32[]{:S(2)}) collective-permute-start(f32[3,10,8,128]{3,2,1,0:T(8,128)S(1)} %get-tuple-element.24.own_east_ref), channel_id=1, source_target_pairs={{0,1},{1,2},{2,3},{3,4},{4,5},{5,6},{6,7},{7,0},{8,9},{9,10},{10,1... | collective-permute-start | bytes 368648 | tf_op jit(solution)/shard_map/ppermute | solution.py:560

commit v3 on v2

--- a/solution.py
+++ b/solution.py
@@ -5,6 +5,7 @@
 from jax.experimental.pallas import tpu as pltpu
 from jax.sharding import Mesh
 from jax.sharding import PartitionSpec as P
+
 
 ITERS = 6
 SHIFT = (0.375, 0.0, 0.375, 0.0, 0.375, 0.0)
@@ -251,7 +252,7 @@
             diag_ref[q, at8(8 * (t - 1)), :] = rolled(total, 32 * q)
         return 0
 
-    lax.fori_loop(1, TILES - 1, inner_weights, 0, unroll=4)
+    lax.fori_loop(1, TILES - 1, inner_weights, 0, unroll=True)
 
     @pl.when(top_ref[0] == 0)
     def _():
@@ -277,7 +278,7 @@
         first(t, lambda m: right_ref[m, at8(8 * (t - 1)), :])
         return 0
 
-    lax.fori_loop(1, TILES - 1, inner_first, 0, unroll=4)
+    lax.fori_loop(1, TILES - 1, inner_first, 0, unroll=True)
     first(TILES - 1, lambda m: right_halo_ref[m, 1])
 
     def parts(ref, j, base, w):
@@ -307,7 +308,7 @@
 
         def end(values):
             for s, (middle, edge, moved) in enumerate(values):
-                edge_ref[t, s] = edge
+                edge_ref[j % 2, t, s] = edge
                 if moved:
                     strip_ref[j + 1, at8(8 + s * EXT + 8 * t), :] = middle + moved[0] + moved[1]
 
@@ -320,7 +321,7 @@
             values = []
             for s in groups:
                 middle, ahead, behind = parts(basis_ref, j, main_row(4 * s + q, t), w)
-                middle = middle + jnp.where(ends, edge_ref[t, s], 0.0)
+                middle = middle + jnp.where(ends, edge_ref[j % 2, t, s], 0.0)
                 values.append((middle, pltpu.roll(ahead, LANES - 1, 1), pltpu.roll(behind, 1, 1)))
             return values
 
@@ -330,20 +331,21 @@
 
         return begin, end
 
-    for j in range(ITERS):
+    def span(j, n):
         low, high = (0, TILES) if j + 1 < ITERS else (1, TILES - 1)
         half = (high - low) // 2
-
-        def strip_body(n, _, j=j, low=low, half=half):
-            staged([strip_work(j, low + half * n + k) for k in range(half)])
+        return [low + half * n + k for k in range(half)]
+
+    staged([strip_work(0, t) for n in range(2) for t in span(0, n)])
+    for j in range(ITERS):
+        def body(n, _, j=j):
+            work = [main_work(j, t, q, range(GROUPS)) for t in span(j, n) for q in range(4)]
+            if j + 1 < ITERS:
+                work += [strip_work(j + 1, t) for t in span(j + 1, n)]
+            staged(work)
             return 0
 
-        def main_body(n, _, j=j, low=low, half=half):
-            staged([main_work(j, low + half * n + k, q, range(GROUPS)) for k in range(half) for q in range(4)])
-            return 0
-
-        lax.fori_loop(0, 2, strip_body, 0)
-        lax.fori_loop(0, 2, main_body, 0)
+        lax.fori_loop(0, 2, body, 0)
 
     def products(s, _):
         for q in range(4):
@@ -503,7 +505,7 @@
     return jax.ShapeDtypeStruct(dims, F32)
 
 
-def call(kernel, inputs, out_shape, scratch=(), name=None, in_specs=None, out_specs=None):
+def call(kernel, inputs, out_shape, scratch=(), in_specs=None, out_specs=None):
     return pl.pallas_call(
         kernel,
         out_shape=out_shape,
@@ -511,7 +513,6 @@
         out_specs=out_specs or [VMEM] * len(out_shape),
         scratch_shapes=list(scratch),
         interpret=INTERPRET,
-        name=name,
         compiler_params=pltpu.CompilerParams(vmem_limit_bytes=28 * 1024 * 1024),
     )(*inputs)
 
@@ -531,21 +532,17 @@
             pltpu.VMEM((ROWS, LANES), jnp.int32),
             pltpu.SemaphoreType.DMA((5,)),
         ),
-        name="edges",
         in_specs=[HBM] * 4,
     )
-    with jax.named_scope("south"):
-        south = lax.ppermute(last, GY, [(k, k + 1) for k in range(ny - 1)])
-    with jax.named_scope("north"):
-        north = lax.ppermute(first, GY, [(k + 1, k) for k in range(ny - 1)])
+    south = lax.ppermute(last, GY, [(k, k + 1) for k in range(ny - 1)])
+    north = lax.ppermute(first, GY, [(k + 1, k) for k in range(ny - 1)])
     row = (ny - 1) * nx
     turned_last = last[::-1, ::-1]
-    with jax.named_scope("fold"):
-        fold = lax.ppermute(turned_last, ALL, [(row + k, row + nx - 1 - k) for k in range(nx)])
+    fold = lax.ppermute(turned_last, ALL, [(row + k, row + nx - 1 - k) for k in range(nx)])
 
     inner = shape(3, TILES - 2, 8, LANES)
     turned, inner_west, inner_east = call(
-        pack_own_kernel, (right_side, planes), (shape(MEMBERS, ROWS, LANES), inner, inner), name="pack_own",
+        pack_own_kernel, (right_side, planes), (shape(MEMBERS, ROWS, LANES), inner, inner),
         scratch=(pltpu.VMEM((MEMBERS, ROWS, LANES), F32), pltpu.SemaphoreType.DMA),
         in_specs=[HBM, VMEM],
     )
@@ -555,7 +552,6 @@
         (south, north, fold, inner_west, inner_east),
         (shape(MEMBERS, 2, 8, LANES), shape(PLANES, 2, 8, LANES), packed, packed),
         scratch=(pltpu.VMEM((2, MEMBERS, 8, LANES), F32),),
-        name="pack_halo",
     )
     from_west = lax.ppermute(own_east, GX, [(k, (k + 1) % nx) for k in range(nx)])
     from_east = lax.ppermute(own_west, GX, [((k + 1) % nx, k) for k in range(nx)])
@@ -573,10 +569,9 @@
             pltpu.VMEM((TILES, 8, 8, LANES), F32),
             pltpu.VMEM((TILES, 4, 8, LANES), F32),
             pltpu.VMEM((TILES, 8, LANES), F32),
-            pltpu.VMEM((TILES, GROUPS, 8, LANES), F32),
+            pltpu.VMEM((2, TILES, GROUPS, 8, LANES), F32),
             pltpu.VMEM((len(PAIRS) * MEMBERS * 8, LANES), F32),
         ),
-        name="basis",
         in_specs=[SMEM] + [VMEM] * 8,
     )
     parts = lax.all_to_all(gram, NEAR, 0, 0, tiled=True)
@@ -593,7 +588,6 @@
             pltpu.VMEM((MEMBERS, ROWS, LANES), F32),
             pltpu.SemaphoreType.DMA((2, GROUPS)),
         ),
-        name="finish",
         out_specs=[HBM, HBM],
     ))
 

time: 67.4 us -> 67.2 us (level)
  no operation moved by 1% of the time
where the time goes in v3:
time: 67.2 us; the launch traced here: 66.9 us
  blocking collectives  33.7 us (50%)
  Pallas kernels  20.3 us (30%)
  starting transfers between devices  9.73 us (14%)
  waiting for transfers between devices  2.05 us (3%)
  between operations  0.75 us (1%)
    all_to_all x1, blocking collectives, on_device(): parts = lax.all_to_all(gram, NEAR, 0, 0, tiled=True)  24.4 us
    pallas_call x5, Pallas kernels, call(): pl.pallas_call(kernel, out_shape=out_shape, in_specs=in_specs or [VMEM] *...  20.3 us
    all_to_all x1, blocking collectives, on_device(): lax.all_to_all(jnp.broadcast_to(mine[None], (far, *mine.shape)), FAR, 0,...  9.34 us
    ppermute x1, starting transfers between devices, on_device(): south = lax.ppermute(last, GY, [(k, k + 1) for k in range(ny - 1)])  4.57 us
    ppermute x1, starting transfers between devices, on_device(): lax.ppermute(own_west, GX, [((k + 1) % nx, k) for k in range(nx)])  3.2 us
    ppermute x1, waiting for transfers between devices, on_device(): lax.ppermute(own_west, GX, [((k + 1) % nx, k) for k in range(nx)])  2.04 us
  transfers between devices with their start and end apart: 5, of which 1 were waited for; matrix products, arithmetic and copies ran while one was open for 0% of the time, Pallas kernels for 4%

profile of v3, /device:TPU:1, one launch (start us, length us, event | category | flops | bytes accessed | tf_op | source)
XLA Modules:
  0.0 66.9 jit_solution(16865331184546498247)
XLA Ops:
  0.6 1.1 %shard_map.59 = (f32[4,64,128]{2,1,0:T(8,128)S(1)}, f32[224,128]{1,0:T(8,128)S(1)}, f32[224,128]{1,0:T(8,128)S(1)}) custom-call(f32[32,64,128]{2,1,0:T(8,128)} %right_hbm_ref.1, f32[3,64,128]{2,1,0:T(8,128)} %couplings_ref.1, f32[64,128]{1,0:T(8,128)} %center_ref.1, s32[64,128]{1,0:T(8,128)} %mask_ref.1), custom_call_target="tpu_custom_call" | custom-call | tf_op jit(solution)/shard_map/pallas_call | solution.py:509
  1.8 0.4 rev.3
  2.1 0.7 collective-permute-start.2
  2.8 1.3 %collective-permute-start.1 = (f32[224,128]{1,0:T(8,128)S(1)}, f32[224,128]{1,0:T(8,128)S(1)}, u32[]{:S(2)}, u32[]{:S(2)}) collective-permute-start(f32[224,128]{1,0:T(8,128)S(1)} %get-tuple-element.18), channel_id=1, source_target_pairs={{8,0},{16,8},{24,16},{32,24},{40,32},{48,40},{56,48},{64,56},{72,6... | collective-permute-start | bytes 344072 | tf_op jit(solution)/shard_map/ppermute | solution.py:538
  4.1 4.6 %collective-permute-start = (f32[224,128]{1,0:T(8,128)S(1)}, f32[224,128]{1,0:T(8,128)S(1)}, u32[]{:S(2)}, u32[]{:S(2)}) collective-permute-start(f32[224,128]{1,0:T(8,128)S(1)} %get-tuple-element.17), channel_id=1, source_target_pairs={{0,8},{8,16},{16,24},{24,32},{32,40},{40,48},{48,56},{56,64},{64,7... | collective-permute-start | bytes 344072 | tf_op jit(solution)/shard_map/ppermute | solution.py:537
  8.7 2.8 %shard_map.60 = (f32[32,64,128]{2,1,0:T(8,128)S(1)}, f32[3,8,8,128]{3,2,1,0:T(8,128)S(1)}, f32[3,8,8,128]{3,2,1,0:T(8,128)S(1)}) custom-call(f32[32,64,128]{2,1,0:T(8,128)} %right_hbm_ref.1, f32[4,64,128]{2,1,0:T(8,128)S(1)} %get-tuple-element.15.planes_ref), custom_call_target="tpu_custom_call" | custom-call | tf_op jit(solution)/shard_map/pallas_call | solution.py:509
  11.5 0.0 collective-permute-done.2.fold_ref
  11.5 0.0 collective-permute-done.1.north_ref
  11.5 0.0 collective-permute-done.south_ref
  11.5 0.8 %shard_map.61 = (f32[32,2,8,128]{3,2,1,0:T(8,128)S(1)}, f32[4,2,8,128]{3,2,1,0:T(8,128)S(1)}, f32[3,10,8,128]{3,2,1,0:T(8,128)S(1)}, f32[3,10,8,128]{3,2,1,0:T(8,128)S(1)}) custom-call(f32[224,128]{1,0:T(8,128)S(1)} %collective-permute-done.south_ref, f32[224,128]{1,0:T(8,128)S(1)} %collective-permute-done.1.north_ref, ...), custom_call_target="tpu_custom_call" | custom-call | tf_op jit(solution)/shard_map/pallas_call | solution.py:509
  12.3 3.2 %collective-permute-start.4 = (f32[3,10,8,128]{3,2,1,0:T(8,128)S(1)}, f32[3,10,8,128]{3,2,1,0:T(8,128)S(1)}, u32[]{:S(2)}, u32[]{:S(2)}) collective-permute-start(f32[3,10,8,128]{3,2,1,0:T(8,128)S(1)} %get-tuple-element.23.own_west_ref), channel_id=1, source_target_pairs={{1,0},{2,1},{3,2},{4,3},{5,4},{6,5},{7,6},{0,7},{9,8},{10,9},{11,1... | collective-permute-start | bytes 368648 | tf_op jit(solution)/shard_map/ppermute | solution.py:557
  15.5 0.0 collective-permute-start.3
  15.5 2.0 %collective-permute-done.4.from_east_ref = f32[3,10,8,128]{3,2,1,0:T(8,128)S(1)} collective-permute-done((f32[3,10,8,128]{3,2,1,0:T(8,128)S(1)}, f32[3,10,8,128]{3,2,1,0:T(8,128)S(1)}, u32[]{:S(2)}, u32[]{:S(2)}) %collective-permute-start.4) | collective-permute-done | bytes 122912 | tf_op jit(solution)/shard_map/ppermute | solution.py:557
  17.5 0.0 collective-permute-done.3.from_west_ref
  17.5 12.1 %shard_map.62 = (f32[7,2576,128]{2,1,0:T(8,128)S(1)}, f32[4,64,128]{2,1,0:T(8,128)S(1)}, f32[16,8,128]{2,1,0:T(8,128)S(1)}) custom-call(s32[1]{0:T(128)} %bitcast.top_ref, f32[32,64,128]{2,1,0:T(8,128)S(1)} %get-tuple-element.16.right_ref, f32[32,2,8,128]{3,2,1,0:T(8,128)S(1)} %get-tuple-element.21.right_halo_ref, ...), custom_call_target="tpu_custom_call" | custom-call | tf_op jit(solution)/shard_map/pallas_call | solution.py:509
  29.7 24.4 %all_to_all.10 = f32[16,8,128]{2,1,0:T(8,128)S(1)} all-to-all(f32[16,8,128]{2,1,0:T(8,128)S(1)} %get-tuple-element.25), channel_id=1, replica_groups=mesh['gy_0'=8,'gy_1'=4,'gx_0'=4,'gx_1'=2] {'gy_0','gx_1'}, dimensions={0} | all-to-all | bytes 131072 | tf_op jit(solution)/shard_map/all_to_all | solution.py:577
  54.1 9.3 %all_to_all.11.total_ref = f32[16,2,8,128]{3,2,1,0:T(8,128)S(1)} all-to-all(f32[16,2,8,128]{3,2,1,0:T(8,128)S(1)} %broadcast_in_dim.2), channel_id=1, replica_groups=mesh['gy_0'=8,'gy_1'=4,'gx_0'=4,'gx_1'=2] {'gy_1','gx_0'}, dimensions={0} | all-to-all | bytes 262144 | tf_op jit(solution)/shard_map/all_to_all | solution.py:580
  63.5 3.5 %shard_map.63 = (f32[32,64,128]{2,1,0:T(8,128)}, f32[32,64,128]{2,1,0:T(8,128)}) custom-call(f32[16,2,8,128]{3,2,1,0:T(8,128)S(1)} %all_to_all.11.total_ref, f32[7,2576,128]{2,1,0:T(8,128)S(1)} %get-tuple-element.26.basis_ref, f32[4,64,128]{2,1,0:T(8,128)S(1)} %get-tuple-element.27.diag_ref), custom_call_target="tpu_custom_call" | custom-call | tf_op jit(solution)/shard_map/pallas_call | solution.py:509
  (6 shorter events, 0.1 us)
Async XLA Ops:
  2.1 9.4 %collective-permute-start.2 = (f32[224,128]{1,0:T(8,128)S(1)}, f32[224,128]{1,0:T(8,128)S(1)}, u32[]{:S(2)}, u32[]{:S(2)}) collective-permute-start(f32[224,128]{1,0:T(8,128)S(1)} %rev.3), channel_id=1, source_target_pairs={{248,255},{249,254},{250,253},{251,252},{252,251},{253,250},{254,2... | collective-permute-start | bytes 344072 | tf_op jit(solution)/shard_map/ppermute | solution.py:541
  2.8 8.7 %collective-permute-start.1 = (f32[224,128]{1,0:T(8,128)S(1)}, f32[224,128]{1,0:T(8,128)S(1)}, u32[]{:S(2)}, u32[]{:S(2)}) collective-permute-start(f32[224,128]{1,0:T(8,128)S(1)} %get-tuple-element.18), channel_id=1, source_target_pairs={{8,0},{16,8},{24,16},{32,24},{40,32},{48,40},{56,48},{64,56},{72,6... | collective-permute-start | bytes 344072 | tf_op jit(solution)/shard_map/ppermute | solution.py:538
  4.1 7.4 %collective-permute-start = (f32[224,128]{1,0:T(8,128)S(1)}, f32[224,128]{1,0:T(8,128)S(1)}, u32[]{:S(2)}, u32[]{:S(2)}) collective-permute-start(f32[224,128]{1,0:T(8,128)S(1)} %get-tuple-element.17), channel_id=1, source_target_pairs={{0,8},{8,16},{16,24},{24,32},{32,40},{40,48},{48,56},{56,64},{64,7... | collective-permute-start | bytes 344072 | tf_op jit(solution)/shard_map/ppermute | solution.py:537
  12.3 5.2 %collective-permute-start.4 = (f32[3,10,8,128]{3,2,1,0:T(8,128)S(1)}, f32[3,10,8,128]{3,2,1,0:T(8,128)S(1)}, u32[]{:S(2)}, u32[]{:S(2)}) collective-permute-start(f32[3,10,8,128]{3,2,1,0:T(8,128)S(1)} %get-tuple-element.23.own_west_ref), channel_id=1, source_target_pairs={{1,0},{2,1},{3,2},{4,3},{5,4},{6,5},{7,6},{0,7},{9,8},{10,9},{11,1... | collective-permute-start | bytes 368648 | tf_op jit(solution)/shard_map/ppermute | solution.py:557
  15.5 2.0 %collective-permute-start.3 = (f32[3,10,8,128]{3,2,1,0:T(8,128)S(1)}, f32[3,10,8,128]{3,2,1,0:T(8,128)S(1)}, u32[]{:S(2)}, u32[]{:S(2)}) collective-permute-start(f32[3,10,8,128]{3,2,1,0:T(8,128)S(1)} %get-tuple-element.24.own_east_ref), channel_id=1, source_target_pairs={{0,1},{1,2},{2,3},{3,4},{4,5},{5,6},{6,7},{7,0},{8,9},{9,10},{10,1... | collective-permute-start | bytes 368648 | tf_op jit(solution)/shard_map/ppermute | solution.py:556

commit v4 on v3

--- a/solution.py
+++ b/solution.py
@@ -110,11 +110,12 @@
 
 
 def pack_halo_kernel(
-    south_ref, north_ref, fold_ref, own_west_ref, own_east_ref, turned_ref, planes_ref, west_ref, east_ref, rows_ref
+    south_ref, north_ref, fold_ref, own_west_ref, own_east_ref, turned_ref, planes_ref, west_ref, east_ref, rows_ref,
+    ends_west_ref, ends_east_ref,
 ):
-    for h in range(3):
-        west_ref[h, 1 : TILES - 1] = own_west_ref[h]
-        east_ref[h, 1 : TILES - 1] = own_east_ref[h]
+    for h in range(2):
+        west_ref[TILES * h + 1 : TILES * (h + 1) - 1] = own_west_ref[h]
+        east_ref[TILES * h + 1 : TILES * (h + 1) - 1] = own_east_ref[h]
     zero = jnp.zeros((8, LANES), F32)
     for m in range(MEMBERS):
         rows_ref[0, m] = zero
@@ -134,7 +135,19 @@
         def store(m, value, k=k):
             turned_ref[m, k] = value
 
-        pack(load, store, west_ref, east_ref, tile)
+        pack(load, store, ends_west_ref, ends_east_ref, k)
+        for h in range(2):
+            west_ref[TILES * h + tile] = ends_west_ref[h, k]
+            east_ref[TILES * h + tile] = ends_east_ref[h, k]
+    part = lanes_of() % 32 // 8
+    for out_ref, own_ref, ends_ref in ((west_ref, own_west_ref, ends_west_ref), (east_ref, own_east_ref, ends_east_ref)):
+        for n in range((TILES + 3) // 4):
+            value = None
+            for tile in range(4 * n, min(4 * n + 4, TILES)):
+                one = ends_ref[2, 0] if tile == 0 else ends_ref[2, 1] if tile == TILES - 1 else own_ref[2, tile - 1]
+                one = rolled(one, 8 * (tile % 4))
+                value = one if value is None else jnp.where(part == tile % 4, one, value)
+            out_ref[2 * TILES + n] = value
 
 
 def basis_kernel(
@@ -170,22 +183,19 @@
     plane_strip_ref[0:8] = zero
     plane_strip_ref[8 + PLANES * EXT : 16 + PLANES * EXT] = zero
 
-    def joined(h, tile, at):
-        out = rolled(from_west_ref[h, tile], -7 - at)
-        out = jnp.where(spot < 8, out, rolled(own_west_ref[h, tile], 1 - at))
-        out = jnp.where(spot < 16, out, rolled(own_east_ref[h, tile], 9 - at))
-        return jnp.where(spot < 24, out, rolled(from_east_ref[h, tile], 17 - at))
-
-    def plane_strips(t, _):
-        value = joined(2, t, 0)
+    def joined(n, at):
+        out = rolled(from_west_ref[n], -7 - at)
+        out = jnp.where(spot < 8, out, rolled(own_west_ref[n], 1 - at))
+        out = jnp.where(spot < 16, out, rolled(own_east_ref[n], 9 - at))
+        return jnp.where(spot < 24, out, rolled(from_east_ref[n], 17 - at))
+
+    for t in range(TILES):
+        value = joined(2 * TILES + t // 4, 8 * (t % 4))
         for p in range(PLANES):
             one = jnp.where((lane + 7) // 32 % 4 == p, value, 0.0)
             one = one + pltpu.roll(one, 32, 1)
             one = one + pltpu.roll(one, 64, 1)
-            plane_strip_ref[at8(8 + p * EXT + 8 * t), :] = one
-        return 0
-
-    lax.fori_loop(0, TILES, plane_strips, 0, unroll=True)
+            plane_strip_ref[8 + p * EXT + 8 * t : 16 + p * EXT + 8 * t] = one
 
     def weights(t, ghost):
         dr = 1 if ghost else -1
@@ -270,7 +280,7 @@
                 basis_ref[0, at8(main_row(m, t)), :] = load(m) * inv
         inv = inverse_strip_ref[t]
         for s in range(GROUPS):
-            strip_ref[0, at8(8 + s * EXT + 8 * t), :] = joined(s // 4, t, 8 * (s % 4)) * inv
+            strip_ref[0, at8(8 + s * EXT + 8 * t), :] = joined(TILES * (s // 4) + t, 8 * (s % 4)) * inv
 
     first(0, lambda m: right_halo_ref[m, 0])
 
@@ -495,7 +505,7 @@
             for n, (source, target) in enumerate(((solution_ref, solved_ref), (residual_ref, left_ref)))
         ]
 
-    lax.fori_loop(0, GROUPS, combine, 0, unroll=2)
+    lax.fori_loop(0, GROUPS, combine, 0, unroll=4)
     for s in range(GROUPS):
         for copy in copies(s):
             copy.wait()
@@ -546,12 +556,16 @@
         scratch=(pltpu.VMEM((MEMBERS, ROWS, LANES), F32), pltpu.SemaphoreType.DMA),
         in_specs=[HBM, VMEM],
     )
-    packed = shape(3, TILES, 8, LANES)
+    packed = shape(2 * TILES + (TILES + 3) // 4, 8, LANES)
     turned_halo, planes_halo, own_west, own_east = call(
         pack_halo_kernel,
         (south, north, fold, inner_west, inner_east),
         (shape(MEMBERS, 2, 8, LANES), shape(PLANES, 2, 8, LANES), packed, packed),
-        scratch=(pltpu.VMEM((2, MEMBERS, 8, LANES), F32),),
+        scratch=(
+            pltpu.VMEM((2, MEMBERS, 8, LANES), F32),
+            pltpu.VMEM((3, 2, 8, LANES), F32),
+            pltpu.VMEM((3, 2, 8, LANES), F32),
+        ),
     )
     from_west = lax.ppermute(own_east, GX, [(k, (k + 1) % nx) for k in range(nx)])
     from_east = lax.ppermute(own_west, GX, [((k + 1) % nx, k) for k in range(nx)])

time: 67.2 us -> 67.1 us (level)
  no operation moved by 1% of the time
where the time goes in v4:
time: 67.1 us; the launch traced here: 66.8 us
  blocking collectives  33.7 us (50%)
  Pallas kernels  20.5 us (31%)
  starting transfers between devices  9.73 us (15%)
  waiting for transfers between devices  1.74 us (3%)
  between operations  0.75 us (1%)
    all_to_all x1, blocking collectives, on_device(): parts = lax.all_to_all(gram, NEAR, 0, 0, tiled=True)  24.4 us
    pallas_call x5, Pallas kernels, call(): pl.pallas_call(kernel, out_shape=out_shape, in_specs=in_specs or [VMEM] *...  20.5 us
    all_to_all x1, blocking collectives, on_device(): lax.all_to_all(jnp.broadcast_to(mine[None], (far, *mine.shape)), FAR, 0,...  9.34 us
    ppermute x1, starting transfers between devices, on_device(): south = lax.ppermute(last, GY, [(k, k + 1) for k in range(ny - 1)])  4.57 us
    ppermute x1, starting transfers between devices, on_device(): lax.ppermute(own_west, GX, [((k + 1) % nx, k) for k in range(nx)])  3.2 us
    ppermute x1, waiting for transfers between devices, on_device(): lax.ppermute(own_west, GX, [((k + 1) % nx, k) for k in range(nx)])  1.73 us
  transfers between devices with their start and end apart: 5, of which 1 were waited for; matrix products, arithmetic and copies ran while one was open for 0% of the time, Pallas kernels for 4%

profile of v4, /device:TPU:1, one launch (start us, length us, event | category | flops | bytes accessed | tf_op | source)
XLA Modules:
  0.0 66.8 jit_solution(3172101058928628037)
XLA Ops:
  0.6 1.1 %shard_map.59 = (f32[4,64,128]{2,1,0:T(8,128)S(1)}, f32[224,128]{1,0:T(8,128)S(1)}, f32[224,128]{1,0:T(8,128)S(1)}) custom-call(f32[32,64,128]{2,1,0:T(8,128)} %right_hbm_ref.1, f32[3,64,128]{2,1,0:T(8,128)} %couplings_ref.1, f32[64,128]{1,0:T(8,128)} %center_ref.1, s32[64,128]{1,0:T(8,128)} %mask_ref.1), custom_call_target="tpu_custom_call" | custom-call | tf_op jit(solution)/shard_map/pallas_call | solution.py:519
  1.8 0.4 rev.3
  2.1 0.7 collective-permute-start.2
  2.8 1.3 %collective-permute-start.1 = (f32[224,128]{1,0:T(8,128)S(1)}, f32[224,128]{1,0:T(8,128)S(1)}, u32[]{:S(2)}, u32[]{:S(2)}) collective-permute-start(f32[224,128]{1,0:T(8,128)S(1)} %get-tuple-element.18), channel_id=1, source_target_pairs={{8,0},{16,8},{24,16},{32,24},{40,32},{48,40},{56,48},{64,56},{72,6... | collective-permute-start | bytes 344072 | tf_op jit(solution)/shard_map/ppermute | solution.py:548
  4.1 4.6 %collective-permute-start = (f32[224,128]{1,0:T(8,128)S(1)}, f32[224,128]{1,0:T(8,128)S(1)}, u32[]{:S(2)}, u32[]{:S(2)}) collective-permute-start(f32[224,128]{1,0:T(8,128)S(1)} %get-tuple-element.17), channel_id=1, source_target_pairs={{0,8},{8,16},{16,24},{24,32},{32,40},{40,48},{48,56},{56,64},{64,7... | collective-permute-start | bytes 344072 | tf_op jit(solution)/shard_map/ppermute | solution.py:547
  8.7 2.8 %shard_map.60 = (f32[32,64,128]{2,1,0:T(8,128)S(1)}, f32[3,8,8,128]{3,2,1,0:T(8,128)S(1)}, f32[3,8,8,128]{3,2,1,0:T(8,128)S(1)}) custom-call(f32[32,64,128]{2,1,0:T(8,128)} %right_hbm_ref.1, f32[4,64,128]{2,1,0:T(8,128)S(1)} %get-tuple-element.15.planes_ref), custom_call_target="tpu_custom_call" | custom-call | tf_op jit(solution)/shard_map/pallas_call | solution.py:519
  11.5 0.0 collective-permute-done.2.fold_ref
  11.5 0.0 collective-permute-done.1.north_ref
  11.5 0.0 collective-permute-done.south_ref
  11.5 1.0 %shard_map.61 = (f32[32,2,8,128]{3,2,1,0:T(8,128)S(1)}, f32[4,2,8,128]{3,2,1,0:T(8,128)S(1)}, f32[23,8,128]{2,1,0:T(8,128)S(1)}, f32[23,8,128]{2,1,0:T(8,128)S(1)}) custom-call(f32[224,128]{1,0:T(8,128)S(1)} %collective-permute-done.south_ref, f32[224,128]{1,0:T(8,128)S(1)} %collective-permute-done.1.north_ref, ...), custom_call_target="tpu_custom_call" | custom-call | tf_op jit(solution)/shard_map/pallas_call | solution.py:519
  12.5 3.2 %collective-permute-start.4 = (f32[23,8,128]{2,1,0:T(8,128)S(1)}, f32[23,8,128]{2,1,0:T(8,128)S(1)}, u32[]{:S(2)}, u32[]{:S(2)}) collective-permute-start(f32[23,8,128]{2,1,0:T(8,128)S(1)} %get-tuple-element.23.own_west_ref), channel_id=1, source_target_pairs={{1,0},{2,1},{3,2},{4,3},{5,4},{6,5},{7,6},{0,7},{9,8},{10,9},{11,1... | collective-permute-start | bytes 282632 | tf_op jit(solution)/shard_map/ppermute | solution.py:571
  15.7 0.0 collective-permute-start.3
  15.7 1.7 %collective-permute-done.4.from_east_ref = f32[23,8,128]{2,1,0:T(8,128)S(1)} collective-permute-done((f32[23,8,128]{2,1,0:T(8,128)S(1)}, f32[23,8,128]{2,1,0:T(8,128)S(1)}, u32[]{:S(2)}, u32[]{:S(2)}) %collective-permute-start.4) | collective-permute-done | bytes 94240 | tf_op jit(solution)/shard_map/ppermute | solution.py:571
  17.5 0.0 collective-permute-done.3.from_west_ref
  17.5 12.1 %shard_map.62 = (f32[7,2576,128]{2,1,0:T(8,128)S(1)}, f32[4,64,128]{2,1,0:T(8,128)S(1)}, f32[16,8,128]{2,1,0:T(8,128)S(1)}) custom-call(s32[1]{0:T(128)} %bitcast.top_ref, f32[32,64,128]{2,1,0:T(8,128)S(1)} %get-tuple-element.16.right_ref, f32[32,2,8,128]{3,2,1,0:T(8,128)S(1)} %get-tuple-element.21.right_halo_ref, ...), custom_call_target="tpu_custom_call" | custom-call | tf_op jit(solution)/shard_map/pallas_call | solution.py:519
  29.6 24.4 %all_to_all.10 = f32[16,8,128]{2,1,0:T(8,128)S(1)} all-to-all(f32[16,8,128]{2,1,0:T(8,128)S(1)} %get-tuple-element.25), channel_id=1, replica_groups=mesh['gy_0'=8,'gy_1'=4,'gx_0'=4,'gx_1'=2] {'gy_0','gx_1'}, dimensions={0} | all-to-all | bytes 131072 | tf_op jit(solution)/shard_map/all_to_all | solution.py:591
  54.0 9.3 %all_to_all.11.total_ref = f32[16,2,8,128]{3,2,1,0:T(8,128)S(1)} all-to-all(f32[16,2,8,128]{3,2,1,0:T(8,128)S(1)} %broadcast_in_dim.2), channel_id=1, replica_groups=mesh['gy_0'=8,'gy_1'=4,'gx_0'=4,'gx_1'=2] {'gy_1','gx_0'}, dimensions={0} | all-to-all | bytes 262144 | tf_op jit(solution)/shard_map/all_to_all | solution.py:594
  63.4 3.4 %shard_map.63 = (f32[32,64,128]{2,1,0:T(8,128)}, f32[32,64,128]{2,1,0:T(8,128)}) custom-call(f32[16,2,8,128]{3,2,1,0:T(8,128)S(1)} %all_to_all.11.total_ref, f32[7,2576,128]{2,1,0:T(8,128)S(1)} %get-tuple-element.26.basis_ref, f32[4,64,128]{2,1,0:T(8,128)S(1)} %get-tuple-element.27.diag_ref), custom_call_target="tpu_custom_call" | custom-call | tf_op jit(solution)/shard_map/pallas_call | solution.py:519
  (6 shorter events, 0.1 us)
Async XLA Ops:
  2.1 9.4 %collective-permute-start.2 = (f32[224,128]{1,0:T(8,128)S(1)}, f32[224,128]{1,0:T(8,128)S(1)}, u32[]{:S(2)}, u32[]{:S(2)}) collective-permute-start(f32[224,128]{1,0:T(8,128)S(1)} %rev.3), channel_id=1, source_target_pairs={{248,255},{249,254},{250,253},{251,252},{252,251},{253,250},{254,2... | collective-permute-start | bytes 344072 | tf_op jit(solution)/shard_map/ppermute | solution.py:551
  2.8 8.7 %collective-permute-start.1 = (f32[224,128]{1,0:T(8,128)S(1)}, f32[224,128]{1,0:T(8,128)S(1)}, u32[]{:S(2)}, u32[]{:S(2)}) collective-permute-start(f32[224,128]{1,0:T(8,128)S(1)} %get-tuple-element.18), channel_id=1, source_target_pairs={{8,0},{16,8},{24,16},{32,24},{40,32},{48,40},{56,48},{64,56},{72,6... | collective-permute-start | bytes 344072 | tf_op jit(solution)/shard_map/ppermute | solution.py:548
  4.1 7.4 %collective-permute-start = (f32[224,128]{1,0:T(8,128)S(1)}, f32[224,128]{1,0:T(8,128)S(1)}, u32[]{:S(2)}, u32[]{:S(2)}) collective-permute-start(f32[224,128]{1,0:T(8,128)S(1)} %get-tuple-element.17), channel_id=1, source_target_pairs={{0,8},{8,16},{16,24},{24,32},{32,40},{40,48},{48,56},{56,64},{64,7... | collective-permute-start | bytes 344072 | tf_op jit(solution)/shard_map/ppermute | solution.py:547
  12.5 4.9 %collective-permute-start.4 = (f32[23,8,128]{2,1,0:T(8,128)S(1)}, f32[23,8,128]{2,1,0:T(8,128)S(1)}, u32[]{:S(2)}, u32[]{:S(2)}) collective-permute-start(f32[23,8,128]{2,1,0:T(8,128)S(1)} %get-tuple-element.23.own_west_ref), channel_id=1, source_target_pairs={{1,0},{2,1},{3,2},{4,3},{5,4},{6,5},{7,6},{0,7},{9,8},{10,9},{11,1... | collective-permute-start | bytes 282632 | tf_op jit(solution)/shard_map/ppermute | solution.py:571
  15.7 1.7 %collective-permute-start.3 = (f32[23,8,128]{2,1,0:T(8,128)S(1)}, f32[23,8,128]{2,1,0:T(8,128)S(1)}, u32[]{:S(2)}, u32[]{:S(2)}) collective-permute-start(f32[23,8,128]{2,1,0:T(8,128)S(1)} %get-tuple-element.24.own_east_ref), channel_id=1, source_target_pairs={{0,1},{1,2},{2,3},{3,4},{4,5},{5,6},{6,7},{7,0},{8,9},{9,10},{10,1... | collective-permute-start | bytes 282632 | tf_op jit(solution)/shard_map/ppermute | solution.py:570

commit v5 on v4

--- a/solution.py
+++ b/solution.py
@@ -90,12 +90,16 @@
 
 
 def pack_own_kernel(right_hbm_ref, planes_ref, turned_ref, west_ref, east_ref, right_ref, sem):
-    copy = pltpu.make_async_copy(right_hbm_ref, right_ref, sem)
-    copy.start()
-    copy.wait()
+    def fetch(t):
+        rows = pl.ds(8 * t if isinstance(t, int) else pl.multiple_of(8 * t, 8), 8)
+        return pltpu.make_async_copy(right_hbm_ref.at[:, rows, :], right_ref.at[:, rows, :], sem.at[t])
+
+    for t in range(ROWS // 8):
+        fetch(t).start()
 
     def own(t, _):
         at = pl.multiple_of(8 * t, 8)
+        fetch(t).wait()
 
         def load(m):
             return right_ref[m, pl.ds(at, 8), :] if m < MEMBERS else planes_ref[m - MEMBERS, pl.ds(at, 8), :]
@@ -553,7 +557,7 @@
     inner = shape(3, TILES - 2, 8, LANES)
     turned, inner_west, inner_east = call(
         pack_own_kernel, (right_side, planes), (shape(MEMBERS, ROWS, LANES), inner, inner),
-        scratch=(pltpu.VMEM((MEMBERS, ROWS, LANES), F32), pltpu.SemaphoreType.DMA),
+        scratch=(pltpu.VMEM((MEMBERS, ROWS, LANES), F32), pltpu.SemaphoreType.DMA((ROWS // 8,))),
         in_specs=[HBM, VMEM],
     )
     packed = shape(2 * TILES + (TILES + 3) // 4, 8, LANES)

time: 67.1 us -> 67.1 us (level)
  no operation moved by 1% of the time
where the time goes in v5:
time: 67.1 us; the launch traced here: 66.8 us
  blocking collectives  34 us (51%)
  Pallas kernels  20.2 us (30%)
  starting transfers between devices  9.73 us (15%)
  waiting for transfers between devices  1.74 us (3%)
  between operations  0.75 us (1%)
    all_to_all x1, blocking collectives, on_device(): parts = lax.all_to_all(gram, NEAR, 0, 0, tiled=True)  24.6 us
    pallas_call x5, Pallas kernels, call(): pl.pallas_call(kernel, out_shape=out_shape, in_specs=in_specs or [VMEM] *...  20.2 us
    all_to_all x1, blocking collectives, on_device(): lax.all_to_all(jnp.broadcast_to(mine[None], (far, *mine.shape)), FAR, 0,...  9.34 us
    ppermute x1, starting transfers between devices, on_device(): south = lax.ppermute(last, GY, [(k, k + 1) for k in range(ny - 1)])  4.57 us
    ppermute x1, starting transfers between devices, on_device(): lax.ppermute(own_west, GX, [((k + 1) % nx, k) for k in range(nx)])  3.2 us
    ppermute x1, waiting for transfers between devices, on_device(): lax.ppermute(own_west, GX, [((k + 1) % nx, k) for k in range(nx)])  1.73 us
  transfers between devices with their start and end apart: 5, of which 1 were waited for; matrix products, arithmetic and copies ran while one was open for 0% of the time, Pallas kernels for 4%

profile of v5, /device:TPU:1, one launch (start us, length us, event | category | flops | bytes accessed | tf_op | source)
XLA Modules:
  0.0 66.8 jit_solution(199192126501634072)
XLA Ops:
  0.6 1.1 %shard_map.59 = (f32[4,64,128]{2,1,0:T(8,128)S(1)}, f32[224,128]{1,0:T(8,128)S(1)}, f32[224,128]{1,0:T(8,128)S(1)}) custom-call(f32[32,64,128]{2,1,0:T(8,128)} %right_hbm_ref.1, f32[3,64,128]{2,1,0:T(8,128)} %couplings_ref.1, f32[64,128]{1,0:T(8,128)} %center_ref.1, s32[64,128]{1,0:T(8,128)} %mask_ref.1), custom_call_target="tpu_custom_call" | custom-call | tf_op jit(solution)/shard_map/pallas_call | solution.py:523
  1.8 0.4 rev.3
  2.1 0.7 collective-permute-start.2
  2.8 1.3 %collective-permute-start.1 = (f32[224,128]{1,0:T(8,128)S(1)}, f32[224,128]{1,0:T(8,128)S(1)}, u32[]{:S(2)}, u32[]{:S(2)}) collective-permute-start(f32[224,128]{1,0:T(8,128)S(1)} %get-tuple-element.18), channel_id=1, source_target_pairs={{8,0},{16,8},{24,16},{32,24},{40,32},{48,40},{56,48},{64,56},{72,6... | collective-permute-start | bytes 344072 | tf_op jit(solution)/shard_map/ppermute | solution.py:552
  4.1 4.6 %collective-permute-start = (f32[224,128]{1,0:T(8,128)S(1)}, f32[224,128]{1,0:T(8,128)S(1)}, u32[]{:S(2)}, u32[]{:S(2)}) collective-permute-start(f32[224,128]{1,0:T(8,128)S(1)} %get-tuple-element.17), channel_id=1, source_target_pairs={{0,8},{8,16},{16,24},{24,32},{32,40},{40,48},{48,56},{56,64},{64,7... | collective-permute-start | bytes 344072 | tf_op jit(solution)/shard_map/ppermute | solution.py:551
  8.7 2.5 %shard_map.60 = (f32[32,64,128]{2,1,0:T(8,128)S(1)}, f32[3,8,8,128]{3,2,1,0:T(8,128)S(1)}, f32[3,8,8,128]{3,2,1,0:T(8,128)S(1)}) custom-call(f32[32,64,128]{2,1,0:T(8,128)} %right_hbm_ref.1, f32[4,64,128]{2,1,0:T(8,128)S(1)} %get-tuple-element.15.planes_ref), custom_call_target="tpu_custom_call" | custom-call | tf_op jit(solution)/shard_map/pallas_call | solution.py:523
  11.2 0.0 collective-permute-done.2.fold_ref
  11.2 0.0 collective-permute-done.1.north_ref
  11.3 0.0 collective-permute-done.south_ref
  11.3 1.0 %shard_map.61 = (f32[32,2,8,128]{3,2,1,0:T(8,128)S(1)}, f32[4,2,8,128]{3,2,1,0:T(8,128)S(1)}, f32[23,8,128]{2,1,0:T(8,128)S(1)}, f32[23,8,128]{2,1,0:T(8,128)S(1)}) custom-call(f32[224,128]{1,0:T(8,128)S(1)} %collective-permute-done.south_ref, f32[224,128]{1,0:T(8,128)S(1)} %collective-permute-done.1.north_ref, ...), custom_call_target="tpu_custom_call" | custom-call | tf_op jit(solution)/shard_map/pallas_call | solution.py:523
  12.3 3.2 %collective-permute-start.4 = (f32[23,8,128]{2,1,0:T(8,128)S(1)}, f32[23,8,128]{2,1,0:T(8,128)S(1)}, u32[]{:S(2)}, u32[]{:S(2)}) collective-permute-start(f32[23,8,128]{2,1,0:T(8,128)S(1)} %get-tuple-element.23.own_west_ref), channel_id=1, source_target_pairs={{1,0},{2,1},{3,2},{4,3},{5,4},{6,5},{7,6},{0,7},{9,8},{10,9},{11,1... | collective-permute-start | bytes 282632 | tf_op jit(solution)/shard_map/ppermute | solution.py:575
  15.4 0.0 collective-permute-start.3
  15.5 1.7 %collective-permute-done.4.from_east_ref = f32[23,8,128]{2,1,0:T(8,128)S(1)} collective-permute-done((f32[23,8,128]{2,1,0:T(8,128)S(1)}, f32[23,8,128]{2,1,0:T(8,128)S(1)}, u32[]{:S(2)}, u32[]{:S(2)}) %collective-permute-start.4) | collective-permute-done | bytes 94240 | tf_op jit(solution)/shard_map/ppermute | solution.py:575
  17.2 0.0 collective-permute-done.3.from_west_ref
  17.2 12.1 %shard_map.62 = (f32[7,2576,128]{2,1,0:T(8,128)S(1)}, f32[4,64,128]{2,1,0:T(8,128)S(1)}, f32[16,8,128]{2,1,0:T(8,128)S(1)}) custom-call(s32[1]{0:T(128)} %bitcast.top_ref, f32[32,64,128]{2,1,0:T(8,128)S(1)} %get-tuple-element.16.right_ref, f32[32,2,8,128]{3,2,1,0:T(8,128)S(1)} %get-tuple-element.21.right_halo_ref, ...), custom_call_target="tpu_custom_call" | custom-call | tf_op jit(solution)/shard_map/pallas_call | solution.py:523
  29.3 24.6 %all_to_all.10 = f32[16,8,128]{2,1,0:T(8,128)S(1)} all-to-all(f32[16,8,128]{2,1,0:T(8,128)S(1)} %get-tuple-element.25), channel_id=1, replica_groups=mesh['gy_0'=8,'gy_1'=4,'gx_0'=4,'gx_1'=2] {'gy_0','gx_1'}, dimensions={0} | all-to-all | bytes 131072 | tf_op jit(solution)/shard_map/all_to_all | solution.py:595
  54.0 9.3 %all_to_all.11.total_ref = f32[16,2,8,128]{3,2,1,0:T(8,128)S(1)} all-to-all(f32[16,2,8,128]{3,2,1,0:T(8,128)S(1)} %broadcast_in_dim.2), channel_id=1, replica_groups=mesh['gy_0'=8,'gy_1'=4,'gx_0'=4,'gx_1'=2] {'gy_1','gx_0'}, dimensions={0} | all-to-all | bytes 262144 | tf_op jit(solution)/shard_map/all_to_all | solution.py:598
  63.4 3.4 %shard_map.63 = (f32[32,64,128]{2,1,0:T(8,128)}, f32[32,64,128]{2,1,0:T(8,128)}) custom-call(f32[16,2,8,128]{3,2,1,0:T(8,128)S(1)} %all_to_all.11.total_ref, f32[7,2576,128]{2,1,0:T(8,128)S(1)} %get-tuple-element.26.basis_ref, f32[4,64,128]{2,1,0:T(8,128)S(1)} %get-tuple-element.27.diag_ref), custom_call_target="tpu_custom_call" | custom-call | tf_op jit(solution)/shard_map/pallas_call | solution.py:523
  (6 shorter events, 0.1 us)
Async XLA Ops:
  2.1 9.1 %collective-permute-start.2 = (f32[224,128]{1,0:T(8,128)S(1)}, f32[224,128]{1,0:T(8,128)S(1)}, u32[]{:S(2)}, u32[]{:S(2)}) collective-permute-start(f32[224,128]{1,0:T(8,128)S(1)} %rev.3), channel_id=1, source_target_pairs={{248,255},{249,254},{250,253},{251,252},{252,251},{253,250},{254,2... | collective-permute-start | bytes 344072 | tf_op jit(solution)/shard_map/ppermute | solution.py:555
  2.8 8.4 %collective-permute-start.1 = (f32[224,128]{1,0:T(8,128)S(1)}, f32[224,128]{1,0:T(8,128)S(1)}, u32[]{:S(2)}, u32[]{:S(2)}) collective-permute-start(f32[224,128]{1,0:T(8,128)S(1)} %get-tuple-element.18), channel_id=1, source_target_pairs={{8,0},{16,8},{24,16},{32,24},{40,32},{48,40},{56,48},{64,56},{72,6... | collective-permute-start | bytes 344072 | tf_op jit(solution)/shard_map/ppermute | solution.py:552
  4.1 7.1 %collective-permute-start = (f32[224,128]{1,0:T(8,128)S(1)}, f32[224,128]{1,0:T(8,128)S(1)}, u32[]{:S(2)}, u32[]{:S(2)}) collective-permute-start(f32[224,128]{1,0:T(8,128)S(1)} %get-tuple-element.17), channel_id=1, source_target_pairs={{0,8},{8,16},{16,24},{24,32},{32,40},{40,48},{48,56},{56,64},{64,7... | collective-permute-start | bytes 344072 | tf_op jit(solution)/shard_map/ppermute | solution.py:551
  12.3 4.9 %collective-permute-start.4 = (f32[23,8,128]{2,1,0:T(8,128)S(1)}, f32[23,8,128]{2,1,0:T(8,128)S(1)}, u32[]{:S(2)}, u32[]{:S(2)}) collective-permute-start(f32[23,8,128]{2,1,0:T(8,128)S(1)} %get-tuple-element.23.own_west_ref), channel_id=1, source_target_pairs={{1,0},{2,1},{3,2},{4,3},{5,4},{6,5},{7,6},{0,7},{9,8},{10,9},{11,1... | collective-permute-start | bytes 282632 | tf_op jit(solution)/shard_map/ppermute | solution.py:575
  15.4 1.7 %collective-permute-start.3 = (f32[23,8,128]{2,1,0:T(8,128)S(1)}, f32[23,8,128]{2,1,0:T(8,128)S(1)}, u32[]{:S(2)}, u32[]{:S(2)}) collective-permute-start(f32[23,8,128]{2,1,0:T(8,128)S(1)} %get-tuple-element.24.own_east_ref), channel_id=1, source_target_pairs={{0,1},{1,2},{2,3},{3,4},{4,5},{5,6},{6,7},{7,0},{8,9},{9,10},{10,1... | collective-permute-start | bytes 282632 | tf_op jit(solution)/shard_map/ppermute | solution.py:574
